TPU v7x, 128 devices: a whole 4x4x4 slice. The times are simulated.
128 devices in a mesh: outer: 8 (over z, y_lo), inner: 16 (over y_hi, x, core).
Axes of the slice: x: 4, y: 4 (y_hi: 2, y_lo: 2; y = y_hi * 2 + y_lo), z: 4, core: 2. Of those that a mesh axis runs over, the one named last changes fastest.
Arguments:
- query_gate: bfloat16 [4096, 16384], P(None, ('outer', 'inner')), may hold values from -6 to 6
- key_proj: bfloat16 [4096, 16384], P(None, ('outer', 'inner')), may hold values from -6 to 6
- value_proj: bfloat16 [4096, 16384], P(None, ('outer', 'inner')), may hold values from -6 to 6
- out_grad: bfloat16 [4096, 16384], P(None, ('outer', 'inner')), may hold values from -6 to 6
- filters: float32 [4096, 16384], P(None, ('outer', 'inner')), may hold values from -8 to 8
- skip_bias: float32 [4096], P(('outer', 'inner')), may hold values from -4 to 4
Outputs:
- output: bfloat16 [4096, 16384], P(None, ('outer', 'inner'))
- query_grad: bfloat16 [4096, 16384], P(None, ('outer', 'inner'))
- key_grad: bfloat16 [4096, 16384], P(None, ('outer', 'inner'))
- value_grad: bfloat16 [4096, 16384], P(None, ('outer', 'inner'))
- filter_grad: float32 [4096, 16384], P(None, ('outer', 'inner'))
- bias_grad: float32 [4096], P(('outer', 'inner'))
All inputs are finite; a program needn't handle non-finite values.
Results may differ from a plain program's by a relative error of at most 0.0058.
Values may be sent and summed in bfloat16 or wider, within the bound.
A program may use at most 128 MiB of HBM per device.

v0:
```python
import math

import jax
import jax.numpy as jnp
from jax import lax
from jax.sharding import PartitionSpec as P

PRECISE = lax.Precision.HIGHEST


def dft_tables(length):
    padded_len = 2 * length
    fine_len = min(128, length)
    coarse_len = padded_len // fine_len
    coarse_steps = jnp.arange(coarse_len, dtype=jnp.int32)
    coarse_half = jnp.arange(coarse_len // 2, dtype=jnp.int32)
    fine_steps = jnp.arange(fine_len, dtype=jnp.int32)
    coarse_angle = (coarse_steps[:, None] * coarse_half[None, :] % coarse_len).astype(
        jnp.float32
    ) * (2.0 * math.pi / coarse_len)
    twist_angle = (coarse_steps[:, None] * fine_steps[None, :] % padded_len).astype(jnp.float32) * (
        2.0 * math.pi / padded_len
    )
    fine_angle = (fine_steps[:, None] * fine_steps[None, :] % fine_len).astype(jnp.float32) * (
        2.0 * math.pi / fine_len
    )
    return (
        jnp.cos(coarse_angle),
        jnp.sin(coarse_angle),
        jnp.cos(twist_angle),
        jnp.sin(twist_angle),
        jnp.cos(fine_angle),
        jnp.sin(fine_angle),
    )


def forward_transform(signal, tables):
    cos_coarse, sin_coarse, cos_twist, sin_twist, cos_fine, sin_fine = tables
    channels, length = signal.shape
    fine_len = cos_fine.shape[0]
    blocks = signal.reshape(channels, length // fine_len, fine_len)
    first_real = jnp.einsum("ap,cpr->car", cos_coarse, blocks, precision=PRECISE)
    first_imag = -jnp.einsum("ap,cpr->car", sin_coarse, blocks, precision=PRECISE)
    turned_real = (first_real * cos_twist + first_imag * sin_twist).reshape(-1, fine_len)
    turned_imag = (first_imag * cos_twist - first_real * sin_twist).reshape(-1, fine_len)
    spec_real = jnp.dot(turned_real, cos_fine, precision=PRECISE) + jnp.dot(
        turned_imag, sin_fine, precision=PRECISE
    )
    spec_imag = jnp.dot(turned_imag, cos_fine, precision=PRECISE) - jnp.dot(
        turned_real, sin_fine, precision=PRECISE
    )
    return (spec_real, spec_imag)


def inverse_transform(spec_real, spec_imag, tables, channels):
    cos_coarse, sin_coarse, cos_twist, sin_twist, cos_fine, sin_fine = tables
    fine_len = cos_fine.shape[0]
    coarse_len = cos_coarse.shape[0]
    middle_real = jnp.dot(spec_real, cos_fine, precision=PRECISE) - jnp.dot(
        spec_imag, sin_fine, precision=PRECISE
    )
    middle_imag = jnp.dot(spec_imag, cos_fine, precision=PRECISE) + jnp.dot(
        spec_real, sin_fine, precision=PRECISE
    )
    middle_real = middle_real.reshape(channels, coarse_len, fine_len)
    middle_imag = middle_imag.reshape(channels, coarse_len, fine_len)
    turned_real = middle_real * cos_twist - middle_imag * sin_twist
    turned_imag = middle_imag * cos_twist + middle_real * sin_twist
    result = jnp.einsum("ap,car->cpr", cos_coarse, turned_real, precision=PRECISE) - jnp.einsum(
        "ap,car->cpr", sin_coarse, turned_imag, precision=PRECISE
    )
    return result.reshape(channels, -1) * (1.0 / (coarse_len * fine_len))


def multiply(left_spec, right_spec, conjugate):
    left_real, left_imag = left_spec
    right_real, right_imag = right_spec
    if conjugate:
        return (
            left_real * right_real + left_imag * right_imag,
            left_imag * right_real - left_real * right_imag,
        )
    return (
        left_real * right_real - left_imag * right_imag,
        left_real * right_imag + left_imag * right_real,
    )


def on_device(query_gate, key_proj, value_proj, out_grad, filters, skip_bias):
    mixed_seq = (key_proj.astype(jnp.float32) * value_proj.astype(jnp.float32)).astype(jnp.bfloat16)
    query_wide = query_gate.astype(jnp.float32)
    grad_wide = out_grad.astype(jnp.float32)
    gated_seq = (grad_wide * query_wide).astype(jnp.bfloat16)
    filter_rows = lax.all_to_all(
        filters, ("outer", "inner"), split_axis=0, concat_axis=1, tiled=True
    )
    mixed_rows, gated_rows = (
        lax.all_to_all(mixed_seq, ("outer", "inner"), split_axis=0, concat_axis=1, tiled=True),
        lax.all_to_all(gated_seq, ("outer", "inner"), split_axis=0, concat_axis=1, tiled=True),
    )
    channels, length = mixed_rows.shape
    tables = dft_tables(length)
    filter_spec = forward_transform(filter_rows, tables)
    mixed_wide = mixed_rows.astype(jnp.float32)
    mixed_spec = forward_transform(mixed_wide, tables)
    conv_rows = inverse_transform(*multiply(filter_spec, mixed_spec, False), tables, channels)
    bias_col = skip_bias[:, None]
    convolved_rows = (conv_rows + bias_col * mixed_wide).astype(jnp.bfloat16)
    gated_wide = gated_rows.astype(jnp.float32)
    gated_spec = forward_transform(gated_wide, tables)
    back_rows = inverse_transform(*multiply(gated_spec, filter_spec, True), tables, channels)
    grad_mixed_rows = (back_rows + bias_col * gated_wide).astype(jnp.bfloat16)
    grad_scale = 1.0 / math.sqrt(length)
    filter_rows_grad = (
        inverse_transform(*multiply(gated_spec, mixed_spec, True), tables, channels) * grad_scale
    )
    bias_grad = jnp.sum(gated_wide * mixed_wide, axis=1) * grad_scale
    convolved, mixed_grad = (
        lax.all_to_all(convolved_rows, ("outer", "inner"), split_axis=1, concat_axis=0, tiled=True),
        lax.all_to_all(
            grad_mixed_rows, ("outer", "inner"), split_axis=1, concat_axis=0, tiled=True
        ),
    )
    filter_grad = lax.all_to_all(
        filter_rows_grad.astype(jnp.bfloat16),
        ("outer", "inner"),
        split_axis=1,
        concat_axis=0,
        tiled=True,
    ).astype(filter_rows_grad.dtype)
    conv_wide = convolved.astype(jnp.float32)
    output = (query_wide * conv_wide).astype(jnp.bfloat16)
    query_grad = (grad_wide * conv_wide).astype(jnp.bfloat16)
    grad_wide_mix = mixed_grad.astype(jnp.float32)
    key_grad = (grad_wide_mix * value_proj.astype(jnp.float32)).astype(jnp.bfloat16)
    value_grad = (grad_wide_mix * key_proj.astype(jnp.float32)).astype(jnp.bfloat16)
    return (output, query_grad, key_grad, value_grad, filter_grad, bias_grad)


def solution(mesh):
    return jax.shard_map(
        on_device,
        mesh=mesh,
        in_specs=(
            P(None, ("outer", "inner")),
            P(None, ("outer", "inner")),
            P(None, ("outer", "inner")),
            P(None, ("outer", "inner")),
            P(None, ("outer", "inner")),
            P(("outer", "inner")),
        ),
        out_specs=(
            P(None, ("outer", "inner")),
            P(None, ("outer", "inner")),
            P(None, ("outer", "inner")),
            P(None, ("outer", "inner")),
            P(None, ("outer", "inner")),
            P(("outer", "inner")),
        ),
        check_vma=False,
    )
```

profile of v0, /device:TPU:1, one launch (start us, length us, event | category | flops | bytes accessed | tf_op | source)
XLA Modules:
  0.0 393.6 jit_solution(10821338884738539768)
XLA Ops:
  3.6 11.5 %all-to-all-start.1 = ((bf16[128,32,128]{2,1,0:T(8,128)(2,1)}), bf16[128,32,128]{2,1,0:T(8,128)(2,1)S(1)}, u32[]{:S(2)}, u32[]{:S(2)}) async-start(bf16[128,32,128]{2,1,0:T(8,128)(2,1)} %bitcast.8), calls=%async_computation.1 | async-start | bytes 2097152 | tf_op jit(solution)/shard_map/all_to_all | solution.py:98
  16.3 17.7 %all-to-all-done.1 = bf16[128,32,128]{2,1,0:T(8,128)(2,1)S(1)} async-done(((bf16[128,32,128]{2,1,0:T(8,128)(2,1)}), bf16[128,32,128]{2,1,0:T(8,128)(2,1)S(1)}, u32[]{:S(2)}, u32[]{:S(2)}) %all-to-all-start.1) | async-done | bytes 1048608 | tf_op jit(solution)/shard_map/all_to_all | solution.py:98
  51.4 7.3 %all-to-all-done.3 = bf16[128,32,128]{2,1,0:T(8,128)(2,1)S(1)} async-done(((bf16[128,32,128]{2,1,0:T(8,128)(2,1)}), bf16[128,32,128]{2,1,0:T(8,128)(2,1)S(1)}, u32[]{:S(2)}, u32[]{:S(2)}) %all-to-all-start.3) | async-done | bytes 1048608 | tf_op jit(solution)/shard_map/all_to_all | solution.py:99
  58.7 6.1 %all-to-all-start = ((f32[128,32,128]{2,1,0:T(8,128)}), f32[128,32,128]{2,1,0:T(8,128)}, u32[]{:S(2)}, u32[]{:S(2)}) async-start(f32[128,32,128]{2,1,0:T(8,128)} %bitcast.162), calls=%async_computation | async-start | bytes 4194304 | tf_op jit(solution)/shard_map/all_to_all | solution.py:94
  68.2 9.8 %fusion = (f32[32,256,128]{1,2,0:T(8,128)}, f32[32,256,128]{1,2,0:T(8,128)}, f32[32,256,128]{1,2,0:T(8,128)}, f32[32,256,128]{1,2,0:T(8,128)}) fusion(f32[32,128,256]{2,1,0:T(8,128)S(1)} %fusion.66, f32[256,128]{0,1:T(8,128)S(1)} %copy.41, f32[256,128]{0,1:T(8,128)S(1)} %copy.40, f32[32,128,256]{2,1,0:T(8,128)} %fusion.72, ...), kind=kOutput, calls=%fused_computation.14 | convolution fusion | flops 1625751552 | bytes 30670848 | tf_op jit(solution)/shard_map/ap,cpr->car/dot_general | solution.py:42
  83.6 7.0 %fusion.141 = f32[8192,128]{1,0:T(8,128)} fusion(f32[8192,128]{1,0:T(8,128)} %bitcast.147), kind=kOutput, calls=%fused_computation.158 | convolution fusion | flops 1610842112 | bytes 8388608 | tf_op jit(solution)/shard_map/dot_general | solution.py:46
  101.8 7.2 %fusion.129 = f32[8192,128]{1,0:T(8,128)} fusion(f32[8192,128]{1,0:T(8,128)} %bitcast.153), kind=kOutput, calls=%fused_computation.152 | convolution fusion | flops 1610842112 | bytes 8388608 | tf_op jit(solution)/shard_map/dot_general | solution.py:49
  120.7 7.2 %fusion.131 = f32[8192,128]{1,0:T(8,128)} fusion(f32[8192,128]{1,0:T(8,128)} %bitcast.151), kind=kOutput, calls=%fused_computation.153 | convolution fusion | flops 1610842112 | bytes 8388608 | tf_op jit(solution)/shard_map/dot_general | solution.py:46
  139.0 5.9 %convolution_subtract_fusion.4 = f32[8192,128]{1,0:T(8,128)} fusion(f32[8192,128]{1,0:T(8,128)S(1)} %copy-done.14, f32[8192,128]{1,0:T(8,128)S(1)} %bitcast.148), kind=kOutput, calls=%fused_computation.8 | convolution fusion | flops 1611890688 | bytes 12582912 | tf_op jit(solution)/shard_map/dot_general | solution.py:49
  145.0 6.4 %fusion.39 = f32[256,32,128]{2,0,1:T(8,128)S(1)} fusion(f32[128,32,128]{2,1,0:T(8,128)} %all-to-all-done), kind=kOutput, calls=%fused_computation.76 | convolution fusion | flops 1611071488 | bytes 6291456 | tf_op jit(solution)/shard_map/ap,cpr->car/dot_general | solution.py:43
  151.4 7.2 %multiply_add_fusion.3 = (f32[256,32,128]{2,0,1:T(8,128)S(1)}, f32[256,32,128]{2,0,1:T(8,128)S(1)}) fusion(f32[256,32,128]{2,0,1:T(8,128)S(1)} %fusion.39, f32[256,128]{1,0:T(8,128)S(1)} %get-tuple-element.28, f32[256,128]{1,0:T(8,128)S(1)} %copy-done.27, f32[128,32,128]{2,1,0:T(8,128)} %all-to-all-done), kind=kOutput, calls=%fused_computation.55 | convolution fusion | flops 1618411520 | bytes 14942208 | tf_op jit(solution)/shard_map/ap,cpr->car/dot_general | solution.py:42
  177.1 17.3 %multiply_subtract_fusion = (f32[8192,128]{1,0:T(8,128)}, f32[8192,128]{1,0:T(8,128)}, f32[8192,128]{1,0:T(8,128)}, f32[8192,128]{1,0:T(8,128)}, f32[8192,128]{1,0:T(8,128)}, /*index=5*/f32[8192,128]{1,0:T(8,128)}) fusion(f32[8192,128]{1,0:T(8,128)} %convolution_subtract_fusion.4, f32[8192,128]{1,0:T(8,128)} %convolution_subtract_fusion.2, ...), kind=kOutput, calls=%fused_computation.32 | convolution fusion | flops 1630765056 | bytes 54525952 | tf_op jit(solution)/shard_map/dot_general | solution.py:46
  194.4 6.0 %fusion.121 = f32[8192,128]{1,0:T(8,128)S(1)} fusion(f32[8192,128]{1,0:T(8,128)} %get-tuple-element.6), kind=kOutput, calls=%fused_computation.148 | convolution fusion | flops 1610842112 | bytes 8388608 | tf_op jit(solution)/shard_map/dot_general | solution.py:62
  217.0 8.1 %convolution_subtract_fusion = f32[8192,128]{1,0:T(8,128)} fusion(f32[8192,128]{1,0:T(8,128)} %fusion.123, f32[8192,128]{1,0:T(8,128)} %get-tuple-element.6), kind=kOutput, calls=%fused_computation.1 | convolution fusion | flops 1611890688 | bytes 12582912 | tf_op jit(solution)/shard_map/dot_general | solution.py:59
  230.8 7.1 %fusion.4 = f32[32,128,128]{2,1,0:T(8,128)S(1)} fusion(f32[32,256,128]{1,2,0:T(8,128)} %copy.57, f32[32,256,128]{1,2,0:T(8,128)} %copy.58, f32[256,128]{0,1:T(8,128)S(1)} %copy.41, f32[256,128]{0,1:T(8,128)S(1)} %copy.40), kind=kOutput, calls=%fused_computation.24 | convolution fusion | flops 1614217216 | bytes 10747904 | tf_op jit(solution)/shard_map/ap,car->cpr/dot_general | solution.py:69
  243.6 10.2 %all-to-all-start.5 = ((bf16[32,128,128]{2,0,1:T(8,128)(2,1)}), bf16[32,128,128]{2,0,1:T(8,128)(2,1)S(1)}, u32[]{:S(2)}, u32[]{:S(2)}) async-start(bf16[32,128,128]{2,0,1:T(8,128)(2,1)} %copy.61), calls=%async_computation.5 | async-start | bytes 2097152 | tf_op jit(solution)/shard_map/all_to_all | solution.py:124
  253.8 6.0 %fusion.125 = f32[8192,128]{1,0:T(8,128)S(1)} fusion(f32[8192,128]{1,0:T(8,128)} %get-tuple-element.21), kind=kOutput, calls=%fused_computation.150 | convolution fusion | flops 1610842112 | bytes 8388608 | tf_op jit(solution)/shard_map/dot_general | solution.py:62
  276.4 7.6 %convolution_subtract_fusion.1 = f32[8192,128]{1,0:T(8,128)} fusion(f32[8192,128]{1,0:T(8,128)} %fusion.127, f32[8192,128]{1,0:T(8,128)} %get-tuple-element.21), kind=kOutput, calls=%fused_computation.3 | convolution fusion | flops 1611890688 | bytes 12582912 | tf_op jit(solution)/shard_map/dot_general | solution.py:59
  289.6 6.4 %fusion.133 = f32[8192,128]{1,0:T(8,128)S(1)} fusion(f32[8192,128]{1,0:T(8,128)} %get-tuple-element.19), kind=kOutput, calls=%fused_computation.154 | convolution fusion | flops 1610842112 | bytes 8388608 | tf_op jit(solution)/shard_map/dot_general | solution.py:62
  318.4 6.2 %fusion.135 = f32[8192,128]{1,0:T(8,128)S(1)} fusion(f32[8192,128]{1,0:T(8,128)} %get-tuple-element.18), kind=kOutput, calls=%fused_computation.155 | convolution fusion | flops 1610842112 | bytes 8388608 | tf_op jit(solution)/shard_map/dot_general | solution.py:59
  335.8 10.2 %all-to-all-start.4 = ((bf16[32,128,128]{2,0,1:T(8,128)(2,1)}), bf16[32,128,128]{2,0,1:T(8,128)(2,1)}, u32[]{:S(2)}, u32[]{:S(2)}) async-start(bf16[32,128,128]{2,0,1:T(8,128)(2,1)} %copy.56), calls=%async_computation.4 | async-start | bytes 2097152 | tf_op jit(solution)/shard_map/all_to_all | solution.py:120
  346.1 7.1 %fusion.20 = f32[32,128,128]{2,1,0:T(8,128)S(1)} fusion(f32[32,256,128]{1,2,0:T(8,128)} %copy.44, f32[32,256,128]{1,2,0:T(8,128)} %copy.45, f32[256,128]{0,1:T(8,128)S(1)} %copy.41, f32[256,128]{0,1:T(8,128)S(1)} %copy.40), kind=kOutput, calls=%fused_computation.44 | convolution fusion | flops 1614217216 | bytes 10747904 | tf_op jit(solution)/shard_map/ap,car->cpr/dot_general | solution.py:69
  364.7 6.8 %all-to-all-start.2 = ((bf16[32,128,128]{2,0,1:T(8,128)(2,1)}), bf16[32,128,128]{2,0,1:T(8,128)(2,1)}, u32[]{:S(2)}, u32[]{:S(2)}) async-start(bf16[32,128,128]{2,0,1:T(8,128)(2,1)} %copy.48), calls=%async_computation.2 | async-start | bytes 2097152 | tf_op jit(solution)/shard_map/all_to_all | solution.py:119
  377.9 12.1 %all-to-all-done.2 = bf16[32,128,128]{2,0,1:T(8,128)(2,1)} async-done(((bf16[32,128,128]{2,0,1:T(8,128)(2,1)}), bf16[32,128,128]{2,0,1:T(8,128)(2,1)}, u32[]{:S(2)}, u32[]{:S(2)}) %all-to-all-start.2) | async-done | bytes 1048608 | tf_op jit(solution)/shard_map/all_to_all | solution.py:119
  (107 shorter events, 187.9 us)
Async XLA Ops:
  0.6 14.4 %copy-start.22 = (bf16[4096,128]{1,0:T(8,128)(2,1)S(1)}, bf16[4096,128]{1,0:T(8,128)(2,1)}, u32[]{:S(2)}) copy-start(bf16[4096,128]{1,0:T(8,128)(2,1)} %param.6) | copy-start | bytes 3145732
  0.6 14.4 %copy-start.20 = (bf16[4096,128]{1,0:T(8,128)(2,1)S(1)}, bf16[4096,128]{1,0:T(8,128)(2,1)}, u32[]{:S(2)}) copy-start(bf16[4096,128]{1,0:T(8,128)(2,1)} %param.9) | copy-start | bytes 3145732
  3.6 30.4 %all-to-all-start.1 = ((bf16[128,32,128]{2,1,0:T(8,128)(2,1)}), bf16[128,32,128]{2,1,0:T(8,128)(2,1)S(1)}, u32[]{:S(2)}, u32[]{:S(2)}) async-start(bf16[128,32,128]{2,1,0:T(8,128)(2,1)} %bitcast.8), calls=%async_computation.1 | async-start | bytes 2097152 | tf_op jit(solution)/shard_map/all_to_all | solution.py:98
  35.0 23.8 %all-to-all-start.3 = ((bf16[128,32,128]{2,1,0:T(8,128)(2,1)}), bf16[128,32,128]{2,1,0:T(8,128)(2,1)S(1)}, u32[]{:S(2)}, u32[]{:S(2)}) async-start(bf16[128,32,128]{2,1,0:T(8,128)(2,1)} %bitcast.22), calls=%async_computation.3 | async-start | bytes 2097152 | tf_op jit(solution)/shard_map/all_to_all | solution.py:99
  58.7 86.2 %all-to-all-start = ((f32[128,32,128]{2,1,0:T(8,128)}), f32[128,32,128]{2,1,0:T(8,128)}, u32[]{:S(2)}, u32[]{:S(2)}) async-start(f32[128,32,128]{2,1,0:T(8,128)} %bitcast.162), calls=%async_computation | async-start | bytes 4194304 | tf_op jit(solution)/shard_map/all_to_all | solution.py:94
  101.8 7.2 %copy-start.1 = (f32[32,256,128]{2,1,0:T(8,128)S(1)}, f32[32,256,128]{2,1,0:T(8,128)}, u32[]{:S(2)}) copy-start(f32[32,256,128]{2,1,0:T(8,128)} %copy.43) | copy-start | bytes 12582916
  120.7 7.2 %copy-start.2 = (f32[32,256,128]{2,1,0:T(8,128)S(1)}, f32[32,256,128]{2,1,0:T(8,128)}, u32[]{:S(2)}) copy-start(f32[32,256,128]{2,1,0:T(8,128)} %copy.43) | copy-start | bytes 12582916
  120.7 7.2 %copy-start.15 = (f32[8192,128]{1,0:T(8,128)S(1)}, f32[8192,128]{1,0:T(8,128)}, u32[]{:S(2)}) copy-start(f32[8192,128]{1,0:T(8,128)} %fusion.141) | copy-start | bytes 12582916
  144.9 6.5 %copy-start.27 = (f32[256,128]{1,0:T(8,128)S(1)}, f32[256,128]{1,0:T(8,128)}, u32[]{:S(2)}) copy-start(f32[256,128]{1,0:T(8,128)} %copy-done.26) | copy-start | bytes 393220
  230.8 7.1 %copy-start.8 = (f32[32,256,128]{1,2,0:T(8,128)S(1)}, f32[32,256,128]{1,2,0:T(8,128)}, u32[]{:S(2)}) copy-start(f32[32,256,128]{1,2,0:T(8,128)} %copy.58) | copy-start | bytes 12582916
  230.8 7.1 %copy-start.9 = (f32[32,256,128]{1,2,0:T(8,128)S(1)}, f32[32,256,128]{1,2,0:T(8,128)}, u32[]{:S(2)}) copy-start(f32[32,256,128]{1,2,0:T(8,128)} %copy.57) | copy-start | bytes 12582916
  243.6 92.2 %all-to-all-start.5 = ((bf16[32,128,128]{2,0,1:T(8,128)(2,1)}), bf16[32,128,128]{2,0,1:T(8,128)(2,1)S(1)}, u32[]{:S(2)}, u32[]{:S(2)}) async-start(bf16[32,128,128]{2,0,1:T(8,128)(2,1)} %copy.61), calls=%async_computation.5 | async-start | bytes 2097152 | tf_op jit(solution)/shard_map/all_to_all | solution.py:124
  253.8 6.0 %copy-start.6 = (f32[8192,128]{1,0:T(8,128)S(1)}, f32[8192,128]{1,0:T(8,128)}, u32[]{:S(2)}) copy-start(f32[8192,128]{1,0:T(8,128)} %get-tuple-element.20) | copy-start | bytes 12582916
  289.6 6.4 %copy-start.12 = (f32[32,256,128]{1,2,0:T(8,128)S(1)}, f32[32,256,128]{1,2,0:T(8,128)}, u32[]{:S(2)}) copy-start(f32[32,256,128]{1,2,0:T(8,128)} %copy.53) | copy-start | bytes 12582916
  289.6 6.4 %copy-start.13 = (f32[32,256,128]{1,2,0:T(8,128)S(1)}, f32[32,256,128]{1,2,0:T(8,128)}, u32[]{:S(2)}) copy-start(f32[32,256,128]{1,2,0:T(8,128)} %copy.52) | copy-start | bytes 12582916
  318.4 6.2 %copy-start.4 = (f32[8192,128]{1,0:T(8,128)S(1)}, f32[8192,128]{1,0:T(8,128)}, u32[]{:S(2)}) copy-start(f32[8192,128]{1,0:T(8,128)} %get-tuple-element.19) | copy-start | bytes 12582916
  335.8 17.4 %copy-start.23 = (bf16[32,128,128]{2,0,1:T(8,128)(2,1)}, bf16[32,128,128]{2,0,1:T(8,128)(2,1)S(1)}, u32[]{:S(2)}) copy-start(bf16[32,128,128]{2,0,1:T(8,128)(2,1)S(1)} %all-to-all-done.5) | copy-start | bytes 3145732
  335.8 28.8 %all-to-all-start.4 = ((bf16[32,128,128]{2,0,1:T(8,128)(2,1)}), bf16[32,128,128]{2,0,1:T(8,128)(2,1)}, u32[]{:S(2)}, u32[]{:S(2)}) async-start(bf16[32,128,128]{2,0,1:T(8,128)(2,1)} %copy.56), calls=%async_computation.4 | async-start | bytes 2097152 | tf_op jit(solution)/shard_map/all_to_all | solution.py:120
  346.1 7.1 %copy-start.10 = (f32[32,256,128]{1,2,0:T(8,128)S(1)}, f32[32,256,128]{1,2,0:T(8,128)}, u32[]{:S(2)}) copy-start(f32[32,256,128]{1,2,0:T(8,128)} %copy.45) | copy-start | bytes 12582916
  346.1 7.1 %copy-start.11 = (f32[32,256,128]{1,2,0:T(8,128)S(1)}, f32[32,256,128]{1,2,0:T(8,128)}, u32[]{:S(2)}) copy-start(f32[32,256,128]{1,2,0:T(8,128)} %copy.44) | copy-start | bytes 12582916
  358.4 16.5 %copy-start.18 = (bf16[4096,128]{1,0:T(8,128)(2,1)S(1)}, bf16[4096,128]{1,0:T(8,128)(2,1)}, u32[]{:S(2)}) copy-start(bf16[4096,128]{1,0:T(8,128)(2,1)} %param.8) | copy-start | bytes 3145732
  358.4 16.5 %copy-start.19 = (bf16[4096,128]{1,0:T(8,128)(2,1)S(1)}, bf16[4096,128]{1,0:T(8,128)(2,1)}, u32[]{:S(2)}) copy-start(bf16[4096,128]{1,0:T(8,128)(2,1)} %param.7) | copy-start | bytes 3145732
  364.7 25.4 %all-to-all-start.2 = ((bf16[32,128,128]{2,0,1:T(8,128)(2,1)}), bf16[32,128,128]{2,0,1:T(8,128)(2,1)}, u32[]{:S(2)}, u32[]{:S(2)}) async-start(bf16[32,128,128]{2,0,1:T(8,128)(2,1)} %copy.48), calls=%async_computation.2 | async-start | bytes 2097152 | tf_op jit(solution)/shard_map/all_to_all | solution.py:119
  372.0 18.1 %copy-start.21 = (bf16[4096,128]{1,0:T(8,128)(2,1)S(1)}, bf16[4096,128]{1,0:T(8,128)(2,1)}, u32[]{:S(2)}) copy-start(bf16[4096,128]{1,0:T(8,128)(2,1)} %param.9) | copy-start | bytes 3145732
  (11 other events, 47.2 us)
where the time goes:
time: 401 us; the launch traced here: 394 us
  matrix products  220 us (55%)
  local copies, waits for them, and re-layouts  67.1 us (17%)
  starting transfers between devices  49.5 us (12%)
  waiting for transfers between devices  40.5 us (10%)
  other arithmetic  14.9 us (4%)
    dot_general x3, matrix products, forward_transform(): jnp.dot(turned_imag, sin_fine, precision=PRECISE)  28.3 us
    dot_general x3, matrix products, forward_transform(): jnp.einsum('ap,cpr->car', cos_coarse, blocks, precision=PRECISE)  21.3 us
    dot_general x3, matrix products, inverse_transform(): jnp.dot(spec_imag, sin_fine, precision=PRECISE)  21.3 us
    dot_general x3, matrix products, inverse_transform(): jnp.einsum('ap,car->cpr', sin_coarse, turned_imag, precision=PRECISE)  18.4 us
    dot_general x3, matrix products, inverse_transform(): jnp.dot(spec_imag, cos_fine, precision=PRECISE)  18.4 us
    dot_general x3, matrix products, forward_transform(): jnp.dot(turned_real, cos_fine, precision=PRECISE)  18 us
    all_to_all x1, waiting for transfers between devices, on_device(): lax.all_to_all(mixed_seq, ('outer', 'inner'), split_axis=0, concat_axis=1...  17.7 us
    dot_general x3, matrix products, inverse_transform(): jnp.dot(spec_real, cos_fine, precision=PRECISE)  17 us
  transfers between devices with their start and end apart: 6, of which 4 were waited for; matrix products, arithmetic and copies ran while one was open for 50% of the time, Pallas kernels for 0%

commit v1 on v0

--- a/solution.py
+++ b/solution.py
@@ -3,6 +3,8 @@
 import jax
 import jax.numpy as jnp
 from jax import lax
+from jax.experimental import pallas as pl
+from jax.experimental.pallas import tpu as pltpu
 from jax.sharding import PartitionSpec as P
 
 PRECISE = lax.Precision.HIGHEST
@@ -86,18 +88,93 @@
     )
 
 
+AXES = ("outer", "inner")
+DEVICES = 128
+
+
+def my_coords():
+    outer = lax.axis_index("outer")
+    inner = lax.axis_index("inner")
+    return outer // 2, (inner // 8) * 2 + outer % 2, (inner // 2) % 4, inner % 2
+
+
+def partner_at(step, coords):
+    z, y, x, core = coords
+    mixed_step = (step * 47) % DEVICES
+    px = (x + mixed_step) % 4
+    pcore = (core + mixed_step // 4) % 2
+    py = (y + mixed_step // 8) % 4
+    pz = (z + mixed_step // 32) % 4
+    return pz * 2 + py % 2, (py // 2) * 8 + px * 2 + pcore
+
+
+def exchange_kernel(src, dst, send_sem, recv_sem, own_sem):
+    coords = my_coords()
+    me = lax.axis_index("outer") * 16 + lax.axis_index("inner")
+    barrier = pltpu.get_barrier_semaphore()
+
+    @pl.loop(1, DEVICES)
+    def _(step):
+        outer, inner = partner_at(step, coords)
+        pl.semaphore_signal(
+            barrier,
+            inc=1,
+            device_id={"outer": outer, "inner": inner},
+            device_id_type=pl.DeviceIdType.MESH,
+        )
+
+    own = pltpu.make_async_copy(src.at[me], dst.at[me], own_sem)
+    own.start()
+    pl.semaphore_wait(barrier, DEVICES - 1)
+
+    @pl.loop(1, DEVICES)
+    def _(step):
+        outer, inner = partner_at(step, coords)
+        pltpu.make_async_remote_copy(
+            src_ref=src.at[outer * 16 + inner],
+            dst_ref=dst.at[me],
+            send_sem=send_sem,
+            recv_sem=recv_sem,
+            device_id={"outer": outer, "inner": inner},
+            device_id_type=pl.DeviceIdType.MESH,
+        ).start()
+
+    own.wait()
+    rest = dst.at[pl.ds(0, DEVICES - 1)]
+    pltpu.make_async_copy(rest, rest, send_sem).wait()
+    pltpu.make_async_copy(rest, rest, recv_sem).wait()
+
+
+def exchange(array, collective_id):
+    return pl.pallas_call(
+        exchange_kernel,
+        out_shape=jax.ShapeDtypeStruct(array.shape, array.dtype),
+        in_specs=[pl.BlockSpec(memory_space=pltpu.HBM)],
+        out_specs=pl.BlockSpec(memory_space=pltpu.HBM),
+        scratch_shapes=[pltpu.SemaphoreType.DMA] * 3,
+        compiler_params=pltpu.CompilerParams(collective_id=collective_id, has_side_effects=True),
+        name="exchange",
+    )(array)
+
+
 def on_device(query_gate, key_proj, value_proj, out_grad, filters, skip_bias):
     mixed_seq = (key_proj.astype(jnp.float32) * value_proj.astype(jnp.float32)).astype(jnp.bfloat16)
     query_wide = query_gate.astype(jnp.float32)
     grad_wide = out_grad.astype(jnp.float32)
     gated_seq = (grad_wide * query_wide).astype(jnp.bfloat16)
-    filter_rows = lax.all_to_all(
-        filters, ("outer", "inner"), split_axis=0, concat_axis=1, tiled=True
-    )
-    mixed_rows, gated_rows = (
-        lax.all_to_all(mixed_seq, ("outer", "inner"), split_axis=0, concat_axis=1, tiled=True),
-        lax.all_to_all(gated_seq, ("outer", "inner"), split_axis=0, concat_axis=1, tiled=True),
-    )
+    packed = jnp.concatenate(
+        [
+            mixed_seq.reshape(DEVICES, 32, 128),
+            gated_seq.reshape(DEVICES, 32, 128),
+            filters.astype(jnp.bfloat16).reshape(DEVICES, 32, 128),
+        ],
+        axis=1,
+    )
+    arrived = exchange(packed, 0)
+    mixed_rows, gated_rows, filter_rows = (
+        arrived[:, 32 * k : 32 * k + 32].transpose(1, 0, 2).reshape(32, -1) for k in range(3)
+    )
+    filter_rows = filter_rows.astype(jnp.float32)
     channels, length = mixed_rows.shape
     tables = dft_tables(length)
     filter_spec = forward_transform(filter_rows, tables)
@@ -115,19 +192,16 @@
         inverse_transform(*multiply(gated_spec, mixed_spec, True), tables, channels) * grad_scale
     )
     bias_grad = jnp.sum(gated_wide * mixed_wide, axis=1) * grad_scale
-    convolved, mixed_grad = (
-        lax.all_to_all(convolved_rows, ("outer", "inner"), split_axis=1, concat_axis=0, tiled=True),
-        lax.all_to_all(
-            grad_mixed_rows, ("outer", "inner"), split_axis=1, concat_axis=0, tiled=True
-        ),
-    )
-    filter_grad = lax.all_to_all(
-        filter_rows_grad.astype(jnp.bfloat16),
-        ("outer", "inner"),
-        split_axis=1,
-        concat_axis=0,
-        tiled=True,
-    ).astype(filter_rows_grad.dtype)
+    results = jnp.concatenate(
+        [
+            rows.reshape(32, DEVICES, 128).transpose(1, 0, 2)
+            for rows in (convolved_rows, grad_mixed_rows, filter_rows_grad.astype(jnp.bfloat16))
+        ],
+        axis=1,
+    )
+    back = exchange(results, 1)
+    convolved, mixed_grad, filter_grad = (back[:, 32 * k : 32 * k + 32].reshape(-1, 128) for k in range(3))
+    filter_grad = filter_grad.astype(jnp.float32)
     conv_wide = convolved.astype(jnp.float32)
     output = (query_wide * conv_wide).astype(jnp.bfloat16)
     query_grad = (grad_wide * conv_wide).astype(jnp.bfloat16)

time: 401 us -> 440 us (1.097)
  Pallas kernels: 0 us -> 99.7 us
  starting transfers between devices: 49.5 us -> 0 us
  waiting for transfers between devices: 40.5 us -> 0 us
  local copies, waits for them, and re-layouts: 67.1 us -> 80 us
  matrix products: 220 us -> 229 us
  other arithmetic: 14.9 us -> 22.8 us
    pallas_call x0 -> x2, Pallas kernels: none -> 99.7 us  [exchange(): pl.pallas_call(exchange_kernel, out_shape=jax.ShapeDtypeStruct(array.shap...]
    all_to_all x6 -> x0, starting transfers between devices: 49.5 us -> none  [the longest x1 11.5 us: on_device(): lax.all_to_all(mixed_seq, ('outer', 'inner'), split_axis=0, concat_axis=1...]
    all_to_all x6 -> x0, waiting for transfers between devices: 40.5 us -> none  [the longest x1 17.7 us: on_device(): lax.all_to_all(mixed_seq, ('outer', 'inner'), split_axis=0, concat_axis=1...]
    dot_general x3, matrix products: 16.9 us -> 30.7 us  [forward_transform(): jnp.dot(turned_real, sin_fine, precision=PRECISE)]
    dot_general x3, matrix products: 14.5 us -> 26.4 us  [inverse_transform(): jnp.einsum('ap,car->cpr', cos_coarse, turned_real, precision=PRECISE)]
    transpose x0 -> x4, local copies, waits for them, and re-layouts: none -> 9.19 us  [on_device(): arrived[:, 32 * k:32 * k + 32].transpose(1, 0, 2).reshape(32, -1)]
    convert_element_type x1 -> x4, other arithmetic: 2.92 us -> 10.3 us  [the longest x1 6.29 us: on_device(): convolved_rows = (conv_rows + bias_col * mixed_wide).astype(jnp.bfloat16)]
    dot_general x3, matrix products: 28.3 us -> 21.3 us  [forward_transform(): jnp.dot(turned_imag, sin_fine, precision=PRECISE)]
  transfers between devices with their start and end apart: 6 -> 0, of which waited for: 4 -> 0; matrix products, arithmetic and copies ran while one was open for 50% -> 0% of each run, Pallas kernels for 0% -> 0%
where the time goes in v1:
time: 440 us; the launch traced here: 433 us
  matrix products  229 us (52%)
  Pallas kernels  99.7 us (23%)
  local copies, waits for them, and re-layouts  80 us (18%)
  other arithmetic  22.8 us (5%)
    pallas_call x2, Pallas kernels, exchange(): pl.pallas_call(exchange_kernel, out_shape=jax.ShapeDtypeStruct(array.shap...  99.7 us
    dot_general x3, matrix products, forward_transform(): jnp.dot(turned_real, sin_fine, precision=PRECISE)  30.7 us
    dot_general x3, matrix products, inverse_transform(): jnp.einsum('ap,car->cpr', cos_coarse, turned_real, precision=PRECISE)  26.4 us
    dot_general x3, matrix products, forward_transform(): jnp.einsum('ap,cpr->car', cos_coarse, blocks, precision=PRECISE)  21.9 us
    dot_general x3, matrix products, forward_transform(): jnp.dot(turned_imag, sin_fine, precision=PRECISE)  21.3 us
    dot_general x3, matrix products, inverse_transform(): jnp.dot(spec_real, cos_fine, precision=PRECISE)  18 us
    dot_general x3, matrix products, forward_transform(): jnp.dot(turned_real, cos_fine, precision=PRECISE)  17.8 us
    reshape x3, local copies, waits for them, and re-layouts, inverse_transform(): middle_real = middle_real.reshape(channels, coarse_len, fine_len)  17.3 us

profile of v1, /device:TPU:1, one launch (start us, length us, event | category | flops | bytes accessed | tf_op | source)
XLA Modules:
  0.0 432.7 jit_solution(13474643215656091970)
XLA Ops:
  6.8 52.2 %exchange.2 = bf16[128,96,128]{2,1,0:T(8,128)(2,1)} custom-call(bf16[128,96,128]{2,1,0:T(8,128)(2,1)} %pad_maximum_fusion.src), custom_call_target="tpu_custom_call" | custom-call | tf_op jit(solution)/shard_map/exchange/pallas_call | solution.py:149
  89.7 13.3 %fusion.4 = (f32[32,256,128]{1,2,0:T(8,128)}, f32[32,256,128]{1,2,0:T(8,128)}, f32[32,256,128]{1,2,0:T(8,128)}, f32[32,256,128]{1,2,0:T(8,128)}, f32[32,256,128]{1,2,0:T(8,128)}, /*index=5*/f32[32,256,128]{1,2,0:T(8,128)}) fusion(f32[32,128,256]{2,1,0:T(8,128)} %fusion.67, f32[256,128]{0,1:T(8,128)S(1)} %get-tuple-element.38, ...), kind=kOutput, calls=%fused_computation.26 | convolution fusion | flops 1633091584 | bytes 47448064 | tf_op jit(solution)/shard_map/ap,cpr->car/dot_general | solution.py:44
  108.5 7.0 %fusion.119 = f32[8192,128]{1,0:T(8,128)} fusion(f32[8192,128]{1,0:T(8,128)} %bitcast.146), kind=kOutput, calls=%fused_computation.157 | convolution fusion | flops 1610842112 | bytes 8388608 | tf_op jit(solution)/shard_map/dot_general | solution.py:48
  115.5 5.7 %copy.61 = f32[32,256,128]{2,1,0:T(8,128)} copy(f32[32,256,128]{1,2,0:T(8,128)} %get-tuple-element.36) | data formatting | bytes 8388608 | tf_op jit(solution)/shard_map/sub | solution.py:47
  121.3 7.8 %convolution_add_fusion.2 = f32[8192,128]{1,0:T(8,128)} fusion(f32[8192,128]{1,0:T(8,128)} %fusion.119, f32[8192,128]{1,0:T(8,128)} %bitcast.150), kind=kOutput, calls=%fused_computation.5 | convolution fusion | flops 1611890688 | bytes 12582912 | tf_op jit(solution)/shard_map/dot_general | solution.py:48
  144.0 7.0 %fusion.125 = f32[8192,128]{1,0:T(8,128)} fusion(f32[8192,128]{1,0:T(8,128)} %bitcast.142), kind=kOutput, calls=%fused_computation.160 | convolution fusion | flops 1610842112 | bytes 8388608 | tf_op jit(solution)/shard_map/dot_general | solution.py:51
  156.7 8.0 %convolution_subtract_fusion.4 = f32[8192,128]{1,0:T(8,128)} fusion(f32[8192,128]{1,0:T(8,128)} %fusion.125, f32[8192,128]{1,0:T(8,128)} %bitcast.144), kind=kOutput, calls=%fused_computation.8 | convolution fusion | flops 1611890688 | bytes 12582912 | tf_op jit(solution)/shard_map/dot_general | solution.py:51
  170.3 7.0 %fusion.131 = f32[8192,128]{1,0:T(8,128)} fusion(f32[8192,128]{1,0:T(8,128)} %bitcast.152), kind=kOutput, calls=%fused_computation.163 | convolution fusion | flops 1610842112 | bytes 8388608 | tf_op jit(solution)/shard_map/dot_general | solution.py:48
  182.9 7.8 %convolution_add_fusion.5 = f32[8192,128]{1,0:T(8,128)} fusion(f32[8192,128]{1,0:T(8,128)} %fusion.131, f32[8192,128]{1,0:T(8,128)} %bitcast.148), kind=kOutput, calls=%fused_computation.11 | convolution fusion | flops 1611890688 | bytes 12582912 | tf_op jit(solution)/shard_map/dot_general | solution.py:48
  194.6 5.7 %convolution_add_fusion.4 = f32[8192,128]{1,0:T(8,128)} fusion(f32[8192,128]{1,0:T(8,128)S(1)} %fusion.129, f32[8192,128]{1,0:T(8,128)S(1)} %bitcast.143), kind=kOutput, calls=%fused_computation.10 | convolution fusion | flops 1611890688 | bytes 12582912 | tf_op jit(solution)/shard_map/dot_general | solution.py:48
  205.7 17.1 %multiply_add_fusion.2 = (f32[8192,128]{1,0:T(8,128)}, f32[8192,128]{1,0:T(8,128)}, f32[8192,128]{1,0:T(8,128)}, f32[8192,128]{1,0:T(8,128)}, f32[8192,128]{1,0:T(8,128)}, /*index=5*/f32[8192,128]{1,0:T(8,128)}) fusion(f32[8192,128]{1,0:T(8,128)} %convolution_add_fusion.4, f32[8192,128]{1,0:T(8,128)} %convolution_add_fusion.5, ...), kind=kOutput, calls=%fused_computation.58 | convolution fusion | flops 1630765056 | bytes 54525952 | tf_op jit(solution)/shard_map/dot_general | solution.py:51
  222.8 6.0 %fusion.113 = f32[8192,128]{1,0:T(8,128)S(1)} fusion(f32[8192,128]{1,0:T(8,128)} %get-tuple-element.21), kind=kOutput, calls=%fused_computation.154 | convolution fusion | flops 1610842112 | bytes 8388608 | tf_op jit(solution)/shard_map/dot_general | solution.py:64
  234.4 5.7 %copy.63 = f32[32,256,128]{1,2,0:T(8,128)} copy(f32[32,256,128]{2,1,0:T(8,128)} %bitcast.157) | data formatting | bytes 8388608 | tf_op jit(solution)/shard_map/reshape | solution.py:68
  240.1 6.0 %fusion.115 = f32[8192,128]{1,0:T(8,128)S(1)} fusion(f32[8192,128]{1,0:T(8,128)} %get-tuple-element.20), kind=kOutput, calls=%fused_computation.155 | convolution fusion | flops 1610842112 | bytes 8388608 | tf_op jit(solution)/shard_map/dot_general | solution.py:61
  251.6 6.0 %copy.62 = f32[32,256,128]{1,2,0:T(8,128)} copy(f32[32,256,128]{2,1,0:T(8,128)} %bitcast.154) | data formatting | bytes 8388608 | tf_op jit(solution)/shard_map/reshape | solution.py:67
  257.6 10.0 %fusion.18 = f32[128,32,128]{2,0,1:T(8,128)} fusion(f32[32,256,128]{1,2,0:T(8,128)} %copy.63, f32[32,256,128]{1,2,0:T(8,128)} %copy.62, f32[256,128]{0,1:T(8,128)S(1)} %get-tuple-element.38, f32[256,128]{0,1:T(8,128)S(1)} %get-tuple-element.39), kind=kOutput, calls=%fused_computation.44 | convolution fusion | flops 1614217216 | bytes 10747904 | tf_op jit(solution)/shard_map/ap,car->cpr/dot_general | solution.py:71
  267.6 6.4 %fusion.14 = f32[128,32,128]{2,0,1:T(8,128)} fusion(f32[32,256,128]{1,2,0:T(8,128)S(1)} %copy-done.17, f32[32,256,128]{1,2,0:T(8,128)S(1)} %copy-done.14, f32[256,128]{0,1:T(8,128)S(1)} %get-tuple-element.38, f32[256,128]{0,1:T(8,128)S(1)} %get-tuple-element.39), kind=kOutput, calls=%fused_computation.40 | convolution fusion | flops 1614217216 | bytes 10747904 | tf_op jit(solution)/shard_map/ap,car->cpr/dot_general | solution.py:71
  283.4 5.7 %copy.49 = f32[32,256,128]{1,2,0:T(8,128)} copy(f32[32,256,128]{2,1,0:T(8,128)} %bitcast.158) | data formatting | bytes 8388608 | tf_op jit(solution)/shard_map/reshape | solution.py:68
  289.1 6.0 %fusion.123 = f32[8192,128]{1,0:T(8,128)S(1)} fusion(f32[8192,128]{1,0:T(8,128)} %get-tuple-element.7), kind=kOutput, calls=%fused_computation.159 | convolution fusion | flops 1610842112 | bytes 8388608 | tf_op jit(solution)/shard_map/dot_general | solution.py:61
  306.2 8.3 %fusion.26 = f32[128,32,128]{2,0,1:T(8,128)S(1)} fusion(f32[32,256,128]{1,2,0:T(8,128)} %copy.49, f32[32,256,128]{1,2,0:T(8,128)} %copy.48, f32[256,128]{0,1:T(8,128)S(1)} %get-tuple-element.38, f32[256,128]{0,1:T(8,128)S(1)} %get-tuple-element.39), kind=kOutput, calls=%fused_computation.54 | convolution fusion | flops 1614217216 | bytes 10747904 | tf_op jit(solution)/shard_map/ap,car->cpr/dot_general | solution.py:71
  319.7 6.3 %fusion.43 = (bf16[128,32,128]{2,1,0:T(8,128)(2,1)}, bf16[128,32,128]{2,1,0:T(8,128)(2,1)}) fusion(f32[128,32,128]{2,0,1:T(8,128)S(1)} %fusion.22, f32[128,32,128]{2,0,1:T(8,128)S(1)} %fusion.26, f32[32]{0:T(128)S(1)} %copy-done.32, bf16[128,96,128]{2,1,0:T(8,128)(2,1)S(1)} %copy-done.19, f32[128,32,128]{2,0,1:T(8,128)S(1)} %copy-done.24, ...), kind=kLoop, calls=%fused_computation.84 | loop fusion | flops 6291456 | bytes 12583040 | tf_op jit(solution)/shard_map/convert_element_type | solution.py:185
  341.4 6.0 %fusion.111 = f32[8192,128]{1,0:T(8,128)S(1)} fusion(f32[8192,128]{1,0:T(8,128)} %get-tuple-element.18), kind=kOutput, calls=%fused_computation.153 | convolution fusion | flops 1610842112 | bytes 8388608 | tf_op jit(solution)/shard_map/dot_general | solution.py:61
  358.6 8.2 %fusion.10 = f32[128,32,128]{2,0,1:T(8,128)S(1)} fusion(f32[32,256,128]{1,2,0:T(8,128)} %copy.71, f32[32,256,128]{1,2,0:T(8,128)} %copy.70, f32[256,128]{0,1:T(8,128)S(1)} %get-tuple-element.38, f32[256,128]{0,1:T(8,128)S(1)} %get-tuple-element.39), kind=kOutput, calls=%fused_computation.34 | convolution fusion | flops 1614217216 | bytes 10747904 | tf_op jit(solution)/shard_map/ap,car->cpr/dot_general | solution.py:71
  376.2 47.5 %exchange.3 = bf16[128,96,128]{2,1,0:T(8,128)(2,1)} custom-call(bf16[128,96,128]{2,1,0:T(8,128)(2,1)} %pad_maximum_fusion.1.src), custom_call_target="tpu_custom_call" | custom-call | tf_op jit(solution)/shard_map/exchange/pallas_call | solution.py:149
  (110 shorter events, 164.8 us)
Async XLA Ops:
  0.6 4.3 copy-start.31
  70.1 4.3 %copy-start.21 = (bf16[32,128,128]{1,2,0:T(8,128)(2,1)}, bf16[32,128,128]{1,2,0:T(8,128)(2,1)S(1)}, u32[]{:S(2)}) copy-start(bf16[32,128,128]{1,2,0:T(8,128)(2,1)S(1)} %copy.42) | copy-start | bytes 3145732
  76.8 8.6 %copy-start.22 = (bf16[32,128,128]{1,2,0:T(8,128)(2,1)S(1)}, bf16[32,128,128]{1,2,0:T(8,128)(2,1)}, u32[]{:S(2)}) copy-start(bf16[32,128,128]{1,2,0:T(8,128)(2,1)} %copy-done.21) | copy-start | bytes 3145732
  81.1 8.6 %copy-start.20 = (f32[32,128,256]{2,1,0:T(8,128)S(1)}, f32[32,128,256]{2,1,0:T(8,128)}, u32[]{:S(2)}) copy-start(f32[32,128,256]{2,1,0:T(8,128)} %fusion.60) | copy-start | bytes 12582916
  121.3 7.8 %copy-start.4 = (f32[32,256,128]{2,1,0:T(8,128)S(1)}, f32[32,256,128]{2,1,0:T(8,128)}, u32[]{:S(2)}) copy-start(f32[32,256,128]{2,1,0:T(8,128)} %copy.61) | copy-start | bytes 12582916
  182.9 7.8 %copy-start.1 = (f32[32,256,128]{2,1,0:T(8,128)S(1)}, f32[32,256,128]{2,1,0:T(8,128)}, u32[]{:S(2)}) copy-start(f32[32,256,128]{2,1,0:T(8,128)} %copy.46) | copy-start | bytes 12582916
  194.6 5.7 %copy-start.3 = (f32[32,256,128]{2,1,0:T(8,128)S(1)}, f32[32,256,128]{2,1,0:T(8,128)}, u32[]{:S(2)}) copy-start(f32[32,256,128]{2,1,0:T(8,128)} %copy.41) | copy-start | bytes 12582916
  222.8 6.0 %copy-start.12 = (f32[8192,128]{1,0:T(8,128)S(1)}, f32[8192,128]{1,0:T(8,128)}, u32[]{:S(2)}) copy-start(f32[8192,128]{1,0:T(8,128)} %get-tuple-element.20) | copy-start | bytes 12582916
  240.1 6.0 %copy-start.11 = (f32[8192,128]{1,0:T(8,128)S(1)}, f32[8192,128]{1,0:T(8,128)}, u32[]{:S(2)}) copy-start(f32[8192,128]{1,0:T(8,128)} %get-tuple-element.21) | copy-start | bytes 12582916
  257.6 10.0 %copy-start.14 = (f32[32,256,128]{1,2,0:T(8,128)S(1)}, f32[32,256,128]{1,2,0:T(8,128)}, u32[]{:S(2)}) copy-start(f32[32,256,128]{1,2,0:T(8,128)} %copy.63) | copy-start | bytes 12582916
  257.6 10.0 %copy-start.17 = (f32[32,256,128]{1,2,0:T(8,128)S(1)}, f32[32,256,128]{1,2,0:T(8,128)}, u32[]{:S(2)}) copy-start(f32[32,256,128]{1,2,0:T(8,128)} %copy.62) | copy-start | bytes 12582916
  267.6 6.4 %copy-start.8 = (f32[8192,128]{1,0:T(8,128)S(1)}, f32[8192,128]{1,0:T(8,128)}, u32[]{:S(2)}) copy-start(f32[8192,128]{1,0:T(8,128)} %get-tuple-element.6) | copy-start | bytes 12582916
  289.1 6.0 %copy-start.9 = (f32[8192,128]{1,0:T(8,128)S(1)}, f32[8192,128]{1,0:T(8,128)}, u32[]{:S(2)}) copy-start(f32[8192,128]{1,0:T(8,128)} %get-tuple-element.6) | copy-start | bytes 12582916
  306.2 8.3 %copy-start.15 = (f32[32,256,128]{1,2,0:T(8,128)S(1)}, f32[32,256,128]{1,2,0:T(8,128)}, u32[]{:S(2)}) copy-start(f32[32,256,128]{1,2,0:T(8,128)} %copy.49) | copy-start | bytes 12582916
  306.2 8.3 %copy-start.18 = (f32[32,256,128]{1,2,0:T(8,128)S(1)}, f32[32,256,128]{1,2,0:T(8,128)}, u32[]{:S(2)}) copy-start(f32[32,256,128]{1,2,0:T(8,128)} %copy.48) | copy-start | bytes 12582916
  314.5 5.1 %copy-start.19 = (bf16[128,96,128]{2,1,0:T(8,128)(2,1)S(1)}, bf16[128,96,128]{2,1,0:T(8,128)(2,1)}, u32[]{:S(2)}) copy-start(bf16[128,96,128]{2,1,0:T(8,128)(2,1)} %exchange.2) | copy-start | bytes 9437188
  314.5 5.1 %copy-start.23 = (f32[128,32,128]{2,0,1:T(8,128)S(1)}, f32[128,32,128]{2,0,1:T(8,128)}, u32[]{:S(2)}) copy-start(f32[128,32,128]{2,0,1:T(8,128)} %fusion.18) | copy-start | bytes 6291460
  314.5 5.1 %copy-start.24 = (f32[128,32,128]{2,0,1:T(8,128)S(1)}, f32[128,32,128]{2,0,1:T(8,128)}, u32[]{:S(2)}) copy-start(f32[128,32,128]{2,0,1:T(8,128)} %fusion.14) | copy-start | bytes 6291460
  314.5 5.1 %copy-start.32 = (f32[32]{0:T(128)S(1)}, f32[32]{0:T(128)}, u32[]{:S(2)}) copy-start(f32[32]{0:T(128)} %param.11) | copy-start | bytes 388
  319.7 6.3 %copy-start.5 = (f32[8192,128]{1,0:T(8,128)S(1)}, f32[8192,128]{1,0:T(8,128)}, u32[]{:S(2)}) copy-start(f32[8192,128]{1,0:T(8,128)} %get-tuple-element.19) | copy-start | bytes 12582916
  326.0 4.2 copy-start.7
  341.4 6.0 %copy-start.6 = (f32[8192,128]{1,0:T(8,128)S(1)}, f32[8192,128]{1,0:T(8,128)}, u32[]{:S(2)}) copy-start(f32[8192,128]{1,0:T(8,128)} %get-tuple-element.19) | copy-start | bytes 12582916
  358.6 8.2 %copy-start.13 = (f32[32,256,128]{1,2,0:T(8,128)S(1)}, f32[32,256,128]{1,2,0:T(8,128)}, u32[]{:S(2)}) copy-start(f32[32,256,128]{1,2,0:T(8,128)} %copy.71) | copy-start | bytes 12582916
  358.6 8.2 %copy-start.16 = (f32[32,256,128]{1,2,0:T(8,128)S(1)}, f32[32,256,128]{1,2,0:T(8,128)}, u32[]{:S(2)}) copy-start(f32[32,256,128]{1,2,0:T(8,128)} %copy.70) | copy-start | bytes 12582916
  (9 other events, 25.6 us)

commit v2 on v1

v2 whole, which is shorter than its diff:
```python
import math, functools
import numpy as np
import jax, jax.numpy as jnp
from jax import lax
from jax.experimental import pallas as pl
from jax.experimental.pallas import tpu as pltpu
from jax.sharding import PartitionSpec as P
BF=jnp.bfloat16; F32=jnp.float32
PITCH=136

def split_np(a):
    hi=np.asarray(a,np.float32).astype(BF)
    lo=(np.asarray(a,np.float64)-np.asarray(hi,np.float64)).astype(np.float32).astype(BF)
    return hi,lo

def tables():
    n=128
    k=np.arange(n)[:,None]; p=np.arange(n)[None,:]
    ang=2*np.pi*((p*(2*k+1))%512)/512
    coarse=np.concatenate([np.cos(ang),-np.sin(ang)],0)
    hi,lo=split_np(coarse)
    fwd_coarse=np.concatenate([hi,lo],1)
    inv=np.concatenate([np.cos(ang),-np.sin(ang)],0).T
    hi,lo=split_np(inv)
    inv_coarse=np.concatenate([hi,lo],1)
    ang=2*np.pi*((k*p)%n)/n
    C,S=np.cos(ang),np.sin(ang)
    fw=np.block([[C,-S],[S,C]])
    iv=np.block([[C,S],[-S,C]])
    hi,lo=split_np(fw); fwd_fine=np.concatenate([hi,lo],0)
    hi,lo=split_np(iv); inv_fine=np.concatenate([hi,lo],0)
    tw=2*np.pi*(p*(2*k+1))/65536.0
    twist=np.concatenate([np.cos(tw),np.sin(tw)],0).astype(np.float32)
    return fwd_coarse,inv_coarse,fwd_fine,inv_fine,twist

def dot(a,b): return jnp.dot(a,b,preferred_element_type=F32)
def split(x):
    hi=x.astype(BF); lo=(x-hi.astype(F32)).astype(BF)
    return hi,lo

def spread(recv, work):
    def body(b,_):
        for u in range(4):
            p=b*4+u
            x=recv[p].astype(F32)
            for j in range(6):
                work[pl.ds(8*j*PITCH+p,8,stride=PITCH),:]=x[8*j:8*j+8]
        return 0
    lax.fori_loop(0,32,body,0)

def gather(work, out):
    def body(b,_):
        for u in range(4):
            p=b*4+u
            x=jnp.concatenate([work[pl.ds(8*j*PITCH+p,8,stride=PITCH),:] for j in range(6)],0)
            out[p]=x.astype(BF)
        return 0
    lax.fori_loop(0,32,body,0)

def transforms(pair, work, bias, bias_out, tabs, zs, fs, chunk):
    fwd_coarse,inv_coarse,fwd_fine,inv_fine,twist=tabs
    tc=twist[:128]; ts=twist[128:]
    rows=lambda s,h: (s*16+2*pair+h)*PITCH
    get=lambda s,h: work[pl.ds(pl.multiple_of(rows(s,h),8),128),:]
    for s in range(3):
        x=jnp.concatenate([get(s,0),get(s,1)],1).astype(BF)
        y=dot(fwd_coarse[...],jnp.concatenate([x,x],0))
        for h in range(2):
            yr=y[:128,128*h:128*h+128]; yi=y[128:,128*h:128*h+128]
            zr=yr*tc+yi*ts; zi=yi*tc-yr*ts
            r0=(2*s+h)*128
            for q,z in enumerate((zr,zi)):
                hi,lo=split(z)
                zs[r0:r0+128,128*q:128*q+128]=hi
                zs[r0:r0+128,256+128*q:384+128*q]=lo
    def fine(w):
        zh=zs[:,:256]; zl=zs[:,256:]
        return dot(zh,w[:256])+dot(zh,w[256:])+dot(zl,w[:256])
    fs[...]=fine(fwd_fine)
    for h in range(2):
        part=lambda s,q: fs[(2*s+h)*128:(2*s+h)*128+128,128*q:128*q+128]
        mr,mi,gr,gi,fr,fi=part(0,0),part(0,1),part(1,0),part(1,1),part(2,0),part(2,1)
        prods=((mr*fr-mi*fi,mr*fi+mi*fr),(gr*fr+gi*fi,gi*fr-gr*fi),(gr*mr+gi*mi,gi*mr-gr*mi))
        for s in range(3):
            r0=(2*s+h)*128
            for q in range(2):
                hi,lo=split(prods[s][q])
                zs[r0:r0+128,128*q:128*q+128]=hi
                zs[r0:r0+128,256+128*q:384+128*q]=lo
    fs[...]=fine(inv_fine)
    ys=[]
    for s in range(3):
        cols_h=[];cols_l=[]
        for h in range(2):
            r0=(2*s+h)*128
            ir=fs[r0:r0+128,:128]; ii=fs[r0:r0+128,128:]
            zr=ir*tc-ii*ts; zi=ii*tc+ir*ts
            rh,rl=split(zr); ih,il=split(zi)
            cols_h.append(jnp.concatenate([rh,ih],0)); cols_l.append(jnp.concatenate([rl,il],0))
        zh=jnp.concatenate(cols_h,1); zl=jnp.concatenate(cols_l,1)
        dh=inv_coarse[:,:256]; dl=inv_coarse[:,256:]
        ys.append(dot(dh,zh)+dot(dl,zh)+dot(dh,zl))
    inv_n=1.0/16384.0
    scale=(inv_n,inv_n,inv_n/128.0)
    for h in range(2):
        ch=chunk*16+2*pair+h
        b=bias[ch]
        m=get(0,h); g=get(1,h)
        bias_out[pl.ds(ch,1),:]=jnp.sum(m*g,axis=0,keepdims=True)*(1.0/128.0)
        vals=[ys[s][:,128*h:128*h+128]*scale[s] for s in range(3)]
        vals[0]=vals[0]+b*m
        vals[1]=vals[1]+b*g
        for s in range(3):
            work[pl.ds(pl.multiple_of(rows(s,h),8),128),:]=vals[s]


AXES = ("outer", "inner")
DEVICES = 128


def my_coords():
    outer = lax.axis_index("outer")
    inner = lax.axis_index("inner")
    return outer // 2, (inner // 8) * 2 + outer % 2, (inner // 2) % 4, inner % 2


def partner_at(step, coords):
    z, y, x, core = coords
    mixed_step = (step * 47) % DEVICES
    px = (x + mixed_step) % 4
    pcore = (core + mixed_step // 4) % 2
    py = (y + mixed_step // 8) % 4
    pz = (z + mixed_step // 32) % 4
    return pz * 2 + py % 2, (py // 2) * 8 + px * 2 + pcore


def send_all(src, dst, send_sem, recv_sem, coords, me):
    @pl.loop(1, DEVICES)
    def _(step):
        outer, inner = partner_at(step, coords)
        pltpu.make_async_remote_copy(
            src_ref=src.at[outer * 16 + inner],
            dst_ref=dst.at[me],
            send_sem=send_sem,
            recv_sem=recv_sem,
            device_id={"outer": outer, "inner": inner},
            device_id_type=pl.DeviceIdType.MESH,
        ).start()


def wait_all(buf, sem):
    rest = buf.at[pl.ds(0, DEVICES - 1)]
    pltpu.make_async_copy(rest, rest, sem).wait()


def hyena_kernel(
    bias, src, fwd_coarse, inv_coarse, fwd_fine, inv_fine, twist,
    out, bias_out,
    recv, back, work, zs, fs,
    send_in, recv_in, send_out, recv_out, own_in, own_out,
):
    coords = my_coords()
    me = lax.axis_index("outer") * 16 + lax.axis_index("inner")
    barrier = pltpu.get_barrier_semaphore()

    @pl.loop(1, DEVICES)
    def _(step):
        outer, inner = partner_at(step, coords)
        pl.semaphore_signal(
            barrier,
            inc=1,
            device_id={"outer": outer, "inner": inner},
            device_id_type=pl.DeviceIdType.MESH,
        )

    own = [
        pltpu.make_async_copy(src.at[half, me], recv.at[half, me], own_in.at[half])
        for half in range(2)
    ]
    for copy in own:
        copy.start()
    pl.semaphore_wait(barrier, DEVICES - 1)
    for half in range(2):
        send_all(src.at[half], recv.at[half], send_in.at[half], recv_in.at[half], coords, me)
    tabs = (fwd_coarse, inv_coarse, fwd_fine, inv_fine, twist)
    own_back = []
    for half in range(2):
        own[half].wait()
        wait_all(recv.at[half], recv_in.at[half])
        spread(recv.at[half], work)

        @pl.loop(0, 8)
        def _(pair):
            transforms(pair, work, bias, bias_out, tabs, zs, fs, half)

        gather(work, back.at[half])
        send_all(back.at[half], out.at[half], send_out.at[half], recv_out.at[half], coords, me)
        own_back.append(pltpu.make_async_copy(back.at[half, me], out.at[half, me], own_out.at[half]))
        own_back[half].start()
    for half in range(2):
        own_back[half].wait()
        wait_all(src.at[half], send_in.at[half])
        wait_all(back.at[half], send_out.at[half])
        wait_all(out.at[half], recv_out.at[half])


def hyena_call(bias, packed):
    vmem = pl.BlockSpec(memory_space=pltpu.VMEM)
    hbm = pl.BlockSpec(memory_space=pltpu.HBM)
    return pl.pallas_call(
        hyena_kernel,
        out_shape=(
            jax.ShapeDtypeStruct((2, DEVICES, 48, 128), BF),
            jax.ShapeDtypeStruct((32, 128), F32),
        ),
        in_specs=[pl.BlockSpec(memory_space=pltpu.SMEM), hbm] + [vmem] * 5,
        out_specs=(hbm, vmem),
        scratch_shapes=[
            pltpu.VMEM((2, DEVICES, 48, 128), BF),
            pltpu.VMEM((2, DEVICES, 48, 128), BF),
            pltpu.VMEM((48 * PITCH, 128), F32),
            pltpu.VMEM((768, 512), BF),
            pltpu.VMEM((768, 256), F32),
        ]
        + [pltpu.SemaphoreType.DMA((2,))] * 6,
        compiler_params=pltpu.CompilerParams(
            collective_id=0, has_side_effects=True, vmem_limit_bytes=40 * 2**20
        ),
        name="hyena",
    )(bias, packed, *[jnp.asarray(t) for t in tables()])


def on_device(query_gate, key_proj, value_proj, out_grad, filters, skip_bias):
    key_wide = key_proj.astype(F32)
    value_wide = value_proj.astype(F32)
    query_wide = query_gate.astype(F32)
    grad_wide = out_grad.astype(F32)
    mixed = (key_wide * value_wide).astype(BF)
    gated = (grad_wide * query_wide).astype(BF)

    def halves(array):
        return array.reshape(DEVICES, 2, 16, 128)

    packed = jnp.concatenate(
        [halves(mixed), halves(gated), halves(filters.astype(BF))], axis=2
    ).transpose(1, 0, 2, 3)
    back, bias_rows = hyena_call(skip_bias, packed)

    def result(k):
        return back[:, :, 16 * k : 16 * k + 16].transpose(1, 0, 2, 3).reshape(-1, 128).astype(F32)

    convolved, mixed_grad, filter_grad = (result(k) for k in range(3))
    return (
        (query_wide * convolved).astype(BF),
        (grad_wide * convolved).astype(BF),
        (mixed_grad * value_wide).astype(BF),
        (mixed_grad * key_wide).astype(BF),
        filter_grad,
        jnp.sum(bias_rows, axis=1),
    )


def solution(mesh):
    wide = P(None, AXES)
    return jax.shard_map(
        on_device,
        mesh=mesh,
        in_specs=(wide, wide, wide, wide, wide, P(AXES)),
        out_specs=(wide, wide, wide, wide, wide, P(AXES)),
        check_vma=False,
    )
```

time: 440 us -> 124 us (0.28)
  the two profiles are of different devices: /device:TPU:1 before, /device:TPU:4 now
where the time goes in v2:
time: 124 us; the launch traced here: 123 us
  Pallas kernels  110 us (89%)
  other arithmetic  6.3 us (5%)
  local copies, waits for them, and re-layouts  6.2 us (5%)
    pallas_call x1, Pallas kernels, hyena_call(): pl.pallas_call(hyena_kernel, out_shape=(jax.ShapeDtypeStruct((2, DEVICES,...  110 us
    unnamed x28, local copies, waits for them, and re-layouts  4.06 us

profile of v2, /device:TPU:4, one launch (start us, length us, event | category | flops | bytes accessed | tf_op | source)
XLA Modules:
  0.0 123.3 jit_solution(14040863399786193378)
XLA Ops:
  0.7 1.8 %convert_element_type.66 = bf16[4096,128]{1,0:T(8,128)(2,1)S(1)} convert(f32[4096,128]{1,0:T(8,128)} %param.15) | non-fusion elementwise | flops 524288 | bytes 3145728 | tf_op jit(solution)/shard_map/convert_element_type | solution.py:245
  2.5 0.3 copy-done.8
  2.8 0.3 fusion.4
  3.1 0.7 copy-done.6
  3.8 0.3 copy-done.12
  4.1 0.3 fusion.2
  4.4 0.0 copy-start
  4.5 0.3 copy_bitcast_fusion.src
  4.7 0.6 copy-done
  5.3 0.1 copy-done.1
  5.4 0.0 copy-done.2
  5.5 0.0 copy-done.3
  5.5 0.0 copy-done.4
  5.5 110.0 %hyena.1 = (bf16[2,128,48,128]{3,2,1,0:T(8,128)(2,1)S(1)}, f32[32,128]{1,0:T(8,128)S(1)}) custom-call(f32[32]{0:T(128)S(1)} %copy-done.5, bf16[2,128,48,128]{3,2,1,0:T(8,128)(2,1)S(1)} %copy_bitcast_fusion.src, bf16[256,256]{1,0:T(8,128)(2,1)S(1)} %copy-done.4, bf16[128,512]{1,0:T(8,128)(2,1)S(1)} %copy-done.3, bf16[512,256]{1,0:T(8,128)(2,1)S(1)} %copy-done.1, ...), custom_call_target="tpu_custom_call" | custom-call | tf_op jit(solution)/shard_map/hyena/pallas_call | solution.py:210
  115.6 0.6 reduce_sum.9
  116.2 0.6 convert_bitcast_fusion
  116.8 1.6 %copy.22 = f32[128,2,16,128]{3,2,1,0:T(8,128)} copy(f32[128,2,16,128]{3,2,0,1:T(8,128)S(1)} %get-tuple-element.10) | data formatting | bytes 4194304 | tf_op jit(solution)/shard_map/convert_element_type | solution.py:250
  118.4 0.2 copy.21
  118.7 0.2 copy.20
  119.0 0.9 copy-done.7
  119.9 0.3 copy-done.9
  120.2 0.3 copy-done.11
  120.6 0.3 copy-done.13
  120.9 2.5 %fusion.1 = (bf16[4096,128]{1,0:T(8,128)(2,1)}, bf16[4096,128]{1,0:T(8,128)(2,1)}, bf16[4096,128]{1,0:T(8,128)(2,1)}, bf16[4096,128]{1,0:T(8,128)(2,1)}) fusion(bf16[4096,128]{1,0:T(8,128)(2,1)S(1)} %copy-done.7, f32[128,2,16,128]{3,2,1,0:T(8,128)S(1)} %copy.21, bf16[4096,128]{1,0:T(8,128)(2,1)S(1)} %copy-done.13, f32[128,2,16,128]{3,2,1,0:T(8,128)S(1)} %copy.20, ...), kind=kLoop, calls=%fused_computation.9 | loop fusion | flops 6291456 | bytes 12582912 | tf_op jit(solution)/shard_map/convert_element_type | solution.py:257
  (15 shorter events, 0.1 us)
Async XLA Ops:
  0.6 1.9 %copy-start.10 = (bf16[4096,128]{1,0:T(8,128)(2,1)S(1)}, bf16[4096,128]{1,0:T(8,128)(2,1)}, u32[]{:S(2)}) copy-start(bf16[4096,128]{1,0:T(8,128)(2,1)} %param.14) | copy-start | bytes 3145732
  0.6 2.2 %copy-start.8 = (bf16[4096,128]{1,0:T(8,128)(2,1)S(1)}, bf16[4096,128]{1,0:T(8,128)(2,1)}, u32[]{:S(2)}) copy-start(bf16[4096,128]{1,0:T(8,128)(2,1)} %param.11) | copy-start | bytes 3145732
  2.5 1.3 %copy-start.6 = (bf16[4096,128]{1,0:T(8,128)(2,1)S(1)}, bf16[4096,128]{1,0:T(8,128)(2,1)}, u32[]{:S(2)}) copy-start(bf16[4096,128]{1,0:T(8,128)(2,1)} %param.12) | copy-start | bytes 3145732
  2.5 1.6 %copy-start.12 = (bf16[4096,128]{1,0:T(8,128)(2,1)S(1)}, bf16[4096,128]{1,0:T(8,128)(2,1)}, u32[]{:S(2)}) copy-start(bf16[4096,128]{1,0:T(8,128)(2,1)} %param.13) | copy-start | bytes 3145732
  4.4 1.0 copy-start
  4.4 1.0 copy-start.1
  4.4 1.0 copy-start.2
  4.4 1.1 copy-start.3
  4.4 1.1 copy-start.4
  4.5 1.1 copy-start.5
  118.7 1.2 copy-start.7
  118.7 1.5 %copy-start.9 = (bf16[4096,128]{1,0:T(8,128)(2,1)S(1)}, bf16[4096,128]{1,0:T(8,128)(2,1)}, u32[]{:S(2)}) copy-start(bf16[4096,128]{1,0:T(8,128)(2,1)} %param.11) | copy-start | bytes 3145732
  118.7 1.8 %copy-start.11 = (bf16[4096,128]{1,0:T(8,128)(2,1)S(1)}, bf16[4096,128]{1,0:T(8,128)(2,1)}, u32[]{:S(2)}) copy-start(bf16[4096,128]{1,0:T(8,128)(2,1)} %param.14) | copy-start | bytes 3145732
  118.7 2.1 %copy-start.13 = (bf16[4096,128]{1,0:T(8,128)(2,1)S(1)}, bf16[4096,128]{1,0:T(8,128)(2,1)}, u32[]{:S(2)}) copy-start(bf16[4096,128]{1,0:T(8,128)(2,1)} %param.13) | copy-start | bytes 3145732

commit v3 on v2

--- a/solution.py
+++ b/solution.py
@@ -104,7 +104,7 @@
     scale=(inv_n,inv_n,inv_n/128.0)
     for h in range(2):
         ch=chunk*16+2*pair+h
-        b=bias[ch]
+        b=bias[0, ch]
         m=get(0,h); g=get(1,h)
         bias_out[pl.ds(ch,1),:]=jnp.sum(m*g,axis=0,keepdims=True)*(1.0/128.0)
         vals=[ys[s][:,128*h:128*h+128]*scale[s] for s in range(3)]
@@ -116,28 +116,28 @@
 
 AXES = ("outer", "inner")
 DEVICES = 128
-
-
-def my_coords():
+BLOCK = 16
+
+
+def partners():
     outer = lax.axis_index("outer")
     inner = lax.axis_index("inner")
-    return outer // 2, (inner // 8) * 2 + outer % 2, (inner // 2) % 4, inner % 2
-
-
-def partner_at(step, coords):
-    z, y, x, core = coords
-    mixed_step = (step * 47) % DEVICES
-    px = (x + mixed_step) % 4
-    pcore = (core + mixed_step // 4) % 2
-    py = (y + mixed_step // 8) % 4
-    pz = (z + mixed_step // 32) % 4
-    return pz * 2 + py % 2, (py // 2) * 8 + px * 2 + pcore
-
-
-def send_all(src, dst, send_sem, recv_sem, coords, me):
-    @pl.loop(1, DEVICES)
-    def _(step):
-        outer, inner = partner_at(step, coords)
+    z, y, x, core = outer // 2, (inner // 8) * 2 + outer % 2, (inner // 2) % 4, inner % 2
+    xs = [(x + k) % 4 for k in range(4)]
+    ys = [(y + k) % 4 for k in range(4)]
+    zs = [(z + k) % 4 for k in range(4)]
+    cores = [(core + k) % 2 for k in range(2)]
+    found = []
+    for step in range(1, DEVICES):
+        mixed_step = (step * 47) % DEVICES
+        px, pcore = xs[mixed_step % 4], cores[mixed_step // 4 % 2]
+        py, pz = ys[mixed_step // 8 % 4], zs[mixed_step // 32]
+        found.append((pz * 2 + py % 2, (py // 2) * 8 + px * 2 + pcore))
+    return found
+
+
+def send_all(src, dst, send_sem, recv_sem, me):
+    for outer, inner in partners():
         pltpu.make_async_remote_copy(
             src_ref=src.at[outer * 16 + inner],
             dst_ref=dst.at[me],
@@ -153,111 +153,168 @@
     pltpu.make_async_copy(rest, rest, sem).wait()
 
 
+def gate(half, key, value, query, grad, filt, packed):
+    @pl.loop(0, DEVICES // 8)
+    def _(group):
+        at = (pl.ds(pl.multiple_of(group * 8, 8), 8), pl.ds(16 * half, 16))
+        put = packed.at[half, at[0]]
+        put[:, :16] = (key[at].astype(F32) * value[at].astype(F32)).astype(BF)
+        put[:, 16:32] = (grad[at].astype(F32) * query[at].astype(F32)).astype(BF)
+        put[:, 32:] = filt[at].astype(BF)
+
+
 def hyena_kernel(
-    bias, src, fwd_coarse, inv_coarse, fwd_fine, inv_fine, twist,
-    out, bias_out,
-    recv, back, work, zs, fs,
-    send_in, recv_in, send_out, recv_out, own_in, own_out,
+    key_in, value_in, query_in, grad_in, filt_in, *rest,
 ):
-    coords = my_coords()
+    tabs_in, rest = rest[:6], rest[6:]
+    out, bias_out, key, value, query, grad = rest[:6]
+    tabs, rest = rest[6:12], rest[12:]
+    filt, packed, recv, back, work, zs, fs, send_in, recv_in, send_out, recv_out, own_out, load = rest
+    bias, tabs = tabs[0], tabs[1:]
     me = lax.axis_index("outer") * 16 + lax.axis_index("inner")
+    loads = [
+        pltpu.make_async_copy(src, dst, load.at[k])
+        for k, (src, dst) in enumerate(
+            (
+                (key_in, key), (value_in, value), (grad_in, grad), (query_in, query), (filt_in, filt),
+                *zip(tabs_in, (bias, *tabs)),
+            )
+        )
+    ]
+    for copy in loads:
+        copy.start()
     barrier = pltpu.get_barrier_semaphore()
-
-    @pl.loop(1, DEVICES)
-    def _(step):
-        outer, inner = partner_at(step, coords)
-        pl.semaphore_signal(
-            barrier,
-            inc=1,
-            device_id={"outer": outer, "inner": inner},
-            device_id_type=pl.DeviceIdType.MESH,
-        )
-
-    own = [
-        pltpu.make_async_copy(src.at[half, me], recv.at[half, me], own_in.at[half])
-        for half in range(2)
-    ]
-    for copy in own:
-        copy.start()
-    pl.semaphore_wait(barrier, DEVICES - 1)
-    for half in range(2):
-        send_all(src.at[half], recv.at[half], send_in.at[half], recv_in.at[half], coords, me)
-    tabs = (fwd_coarse, inv_coarse, fwd_fine, inv_fine, twist)
+    with jax.named_scope("bar_signal"):
+        for outer, inner in partners():
+            pl.semaphore_signal(
+                barrier,
+                inc=1,
+                device_id={"outer": outer, "inner": inner},
+                device_id_type=pl.DeviceIdType.MESH,
+            )
+    with jax.named_scope("loads"):
+        for copy in loads[:5]:
+            copy.wait()
+    with jax.named_scope("gate0"):
+        gate(0, key, value, query, grad, filt, packed)
+    with jax.named_scope("bar_wait"):
+        pl.semaphore_wait(barrier, DEVICES - 1)
+    send_all(packed.at[0], recv.at[0], send_in.at[0], recv_in.at[0], me)
+    recv[0, me] = packed[0, me]
+    with jax.named_scope("gate1"):
+        gate(1, key, value, query, grad, filt, packed)
+    recv[1, me] = packed[1, me]
+    with jax.named_scope("sent_in0"):
+        wait_all(packed.at[0], send_in.at[0])
+    send_all(packed.at[1], recv.at[1], send_in.at[1], recv_in.at[1], me)
+    for copy in loads[5:]:
+        copy.wait()
     own_back = []
     for half in range(2):
-        own[half].wait()
-        wait_all(recv.at[half], recv_in.at[half])
+        with jax.named_scope(f"wait_in{half}"):
+            wait_all(recv.at[half], recv_in.at[half])
         spread(recv.at[half], work)
 
-        @pl.loop(0, 8)
-        def _(pair):
-            transforms(pair, work, bias, bias_out, tabs, zs, fs, half)
+        with jax.named_scope(f"transforms{half}"):
+
+            @pl.loop(0, 8)
+            def _(pair):
+                transforms(pair, work, bias, bias_out, tabs, zs, fs, half)
 
         gather(work, back.at[half])
-        send_all(back.at[half], out.at[half], send_out.at[half], recv_out.at[half], coords, me)
+        with jax.named_scope(f"send_out{half}"):
+            send_all(back.at[half], out.at[half], send_out.at[half], recv_out.at[half], me)
         own_back.append(pltpu.make_async_copy(back.at[half, me], out.at[half, me], own_out.at[half]))
         own_back[half].start()
+    wait_all(packed.at[1], send_in.at[1])
     for half in range(2):
         own_back[half].wait()
-        wait_all(src.at[half], send_in.at[half])
         wait_all(back.at[half], send_out.at[half])
-        wait_all(out.at[half], recv_out.at[half])
-
-
-def hyena_call(bias, packed):
+        with jax.named_scope(f"wait_out{half}"):
+            wait_all(out.at[half], recv_out.at[half])
+
+
+def hyena_call(bias, key, value, query, grad, filt):
+    consts = [jnp.asarray(t) for t in tables()]
     vmem = pl.BlockSpec(memory_space=pltpu.VMEM)
     hbm = pl.BlockSpec(memory_space=pltpu.HBM)
+    rows = jax.ShapeDtypeStruct((DEVICES, 32, 128), BF)
     return pl.pallas_call(
         hyena_kernel,
         out_shape=(
             jax.ShapeDtypeStruct((2, DEVICES, 48, 128), BF),
             jax.ShapeDtypeStruct((32, 128), F32),
+            rows, rows, rows, rows,
         ),
-        in_specs=[pl.BlockSpec(memory_space=pltpu.SMEM), hbm] + [vmem] * 5,
-        out_specs=(hbm, vmem),
-        scratch_shapes=[
+        in_specs=[hbm] * 11,
+        out_specs=(hbm,) + (vmem,) * 5,
+        scratch_shapes=[pltpu.SMEM((1, 32), F32)]
+        + [pltpu.VMEM(t.shape, t.dtype) for t in consts]
+        + [
+            pltpu.VMEM((DEVICES, 32, 128), F32),
+            pltpu.VMEM((2, DEVICES, 48, 128), BF),
             pltpu.VMEM((2, DEVICES, 48, 128), BF),
             pltpu.VMEM((2, DEVICES, 48, 128), BF),
             pltpu.VMEM((48 * PITCH, 128), F32),
             pltpu.VMEM((768, 512), BF),
             pltpu.VMEM((768, 256), F32),
         ]
-        + [pltpu.SemaphoreType.DMA((2,))] * 6,
+        + [pltpu.SemaphoreType.DMA((2,))] * 5
+        + [pltpu.SemaphoreType.DMA((11,))],
         compiler_params=pltpu.CompilerParams(
             collective_id=0, has_side_effects=True, vmem_limit_bytes=40 * 2**20
         ),
         name="hyena",
-    )(bias, packed, *[jnp.asarray(t) for t in tables()])
+    )(
+        *[
+            pltpu.with_memory_space_constraint(t, pltpu.HBM)
+            for t in (key, value, query, grad, filt, bias.reshape(1, 32), *consts)
+        ]
+    )
+
+
+def finish_kernel(back, bias_rows, key, value, query, grad, output, query_grad, key_grad, value_grad, filter_grad, bias_grad):
+    step = pl.program_id(0)
+    at = pl.ds(pl.multiple_of(step * BLOCK, BLOCK), BLOCK)
+    for half in range(2):
+        rows = slice(16 * half, 16 * half + 16)
+        convolved = back[half, at, :16].astype(F32)
+        mixed_grad = back[half, at, 16:32].astype(F32)
+        output[:, rows] = (query[at, rows].astype(F32) * convolved).astype(BF)
+        query_grad[:, rows] = (grad[at, rows].astype(F32) * convolved).astype(BF)
+        key_grad[:, rows] = (value[at, rows].astype(F32) * mixed_grad).astype(BF)
+        value_grad[:, rows] = (key[at, rows].astype(F32) * mixed_grad).astype(BF)
+        filter_grad[:, rows] = back[half, at, 32:].astype(F32)
+
+    @pl.when(step == 0)
+    def _():
+        bias_grad[...] = jnp.sum(bias_rows[...].T, axis=0, keepdims=True)
+
+
+def finish_call(*args):
+    vmem = pl.BlockSpec(memory_space=pltpu.VMEM)
+    block = pl.BlockSpec((BLOCK, 32, 128), lambda i: (i, 0, 0))
+    rows = jax.ShapeDtypeStruct((DEVICES, 32, 128), BF)
+    return pl.pallas_call(
+        finish_kernel,
+        grid=(DEVICES // BLOCK,),
+        out_shape=(rows, rows, rows, rows, jax.ShapeDtypeStruct((DEVICES, 32, 128), F32), jax.ShapeDtypeStruct((1, 32), F32)),
+        in_specs=[vmem] * 6,
+        out_specs=(block,) * 5 + (pl.BlockSpec((1, 32), lambda i: (0, 0)),),
+        compiler_params=pltpu.CompilerParams(vmem_limit_bytes=16 * 2**20),
+        name="finish",
+    )(*args)
 
 
 def on_device(query_gate, key_proj, value_proj, out_grad, filters, skip_bias):
-    key_wide = key_proj.astype(F32)
-    value_wide = value_proj.astype(F32)
-    query_wide = query_gate.astype(F32)
-    grad_wide = out_grad.astype(F32)
-    mixed = (key_wide * value_wide).astype(BF)
-    gated = (grad_wide * query_wide).astype(BF)
-
-    def halves(array):
-        return array.reshape(DEVICES, 2, 16, 128)
-
-    packed = jnp.concatenate(
-        [halves(mixed), halves(gated), halves(filters.astype(BF))], axis=2
-    ).transpose(1, 0, 2, 3)
-    back, bias_rows = hyena_call(skip_bias, packed)
-
-    def result(k):
-        return back[:, :, 16 * k : 16 * k + 16].transpose(1, 0, 2, 3).reshape(-1, 128).astype(F32)
-
-    convolved, mixed_grad, filter_grad = (result(k) for k in range(3))
-    return (
-        (query_wide * convolved).astype(BF),
-        (grad_wide * convolved).astype(BF),
-        (mixed_grad * value_wide).astype(BF),
-        (mixed_grad * key_wide).astype(BF),
-        filter_grad,
-        jnp.sum(bias_rows, axis=1),
+    def rows(array):
+        return array.reshape(DEVICES, 32, 128)
+
+    back, bias_rows, key, value, query, grad = hyena_call(
+        skip_bias, rows(key_proj), rows(value_proj), rows(query_gate), rows(out_grad), rows(filters)
     )
+    *grads, bias_grad = finish_call(back, bias_rows, key, value, query, grad)
+    return (*[array.reshape(-1, 128) for array in grads], bias_grad.reshape(-1))
 
 
 def solution(mesh):

time: 124 us -> 93.1 us (0.75)
  the two profiles are of different devices: /device:TPU:4 before, /device:TPU:1 now
where the time goes in v3:
time: 93.1 us; the launch traced here: 93 us
  Pallas kernels  92.3 us (99%)
    pallas_call x1, Pallas kernels, hyena_call(): pl.pallas_call(hyena_kernel, out_shape=(jax.ShapeDtypeStruct((2, DEVICES,...  88 us
    pallas_call x1, Pallas kernels, finish_call(): pl.pallas_call(finish_kernel, grid=(DEVICES // BLOCK,), out_shape=(rows,...  4.35 us

profile of v3, /device:TPU:1, one launch (start us, length us, event | category | flops | bytes accessed | tf_op | source)
XLA Modules:
  0.0 93.0 jit_solution(17308952290034113288)
XLA Ops:
  0.6 88.0 %hyena.1 = (bf16[2,128,48,128]{3,2,1,0:T(8,128)(2,1)S(1)}, f32[32,128]{1,0:T(8,128)S(1)}, bf16[128,32,128]{2,1,0:T(8,128)(2,1)S(1)}, bf16[128,32,128]{2,1,0:T(8,...) custom-call(bf16[128,32,128]{2,1,0:T(8,128)(2,1)} %bitcast.13, ...), custom_call_target="tpu_custom_call" | custom-call | tf_op jit(solution)/shard_map/hyena/pallas_call | solution.py:242
  88.6 4.3 %finish.1 = (bf16[128,32,128]{2,1,0:T(8,128)(2,1)}, bf16[128,32,128]{2,1,0:T(8,128)(2,1)}, bf16[128,32,128]{2,1,0:T(8,128)(2,1)}, bf16[128,32,128]{2,1,0:T(8,128...) custom-call(bf16[2,128,48,128]{3,2,1,0:T(8,128)(2,1)S(1)} %get-tuple-element.18.back, ...), custom_call_target="tpu_custom_call" | custom-call | tf_op jit(solution)/shard_map/finish/pallas_call | solution.py:298

commit v4 on v3

--- a/solution.py
+++ b/solution.py
@@ -57,61 +57,113 @@
         return 0
     lax.fori_loop(0,32,body,0)
 
-def transforms(pair, work, bias, bias_out, tabs, zs, fs, chunk):
-    fwd_coarse,inv_coarse,fwd_fine,inv_fine,twist=tabs
-    tc=twist[:128]; ts=twist[128:]
-    rows=lambda s,h: (s*16+2*pair+h)*PITCH
-    get=lambda s,h: work[pl.ds(pl.multiple_of(rows(s,h),8),128),:]
+def run_pairs(work, bias, bias_out, tabs, zf, ff, zi, fi, half):
+    fwd_coarse, inv_coarse, fwd_fine, inv_fine, twist = tabs
+    tc = twist[:128]
+    ts = twist[128:]
+
+    def rows(pair, s, h):
+        return pl.ds(pl.multiple_of((s * 16 + 2 * pair + h) * PITCH, 8), 128)
+
+    def put(z, r0, q, value):
+        hi, lo = split(value)
+        z[r0 : r0 + 128, 128 * q : 128 * q + 128] = hi
+        z[r0 : r0 + 128, 256 + 128 * q : 384 + 128 * q] = lo
+
+    def fine(z, f, w, r0, r1):
+        zh = z[r0:r1, :256]
+        f[r0:r1] = dot(zh, w[:256]) + dot(zh, w[256:]) + dot(z[r0:r1, 256:], w[:256])
+
+    def coarse(pair, s):
+        x = jnp.concatenate([work[rows(pair, s, 0), :], work[rows(pair, s, 1), :]], 1).astype(BF)
+        return dot(fwd_coarse[...], jnp.concatenate([x, x], 0))
+
+    def turn(s, y):
+        for h in range(2):
+            yr = y[:128, 128 * h : 128 * h + 128]
+            yi = y[128:, 128 * h : 128 * h + 128]
+            put(zf, (2 * s + h) * 128, 0, yr * tc + yi * ts)
+            put(zf, (2 * s + h) * 128, 1, yi * tc - yr * ts)
+
+    def spectra(s):
+        fine(zf, ff, fwd_fine, 2 * s * 128, 2 * s * 128 + 256)
+
+    def products(h):
+        mr, mi, gr, gi, fr, fi_ = (
+            ff[(2 * s + h) * 128 : (2 * s + h) * 128 + 128, 128 * q : 128 * q + 128]
+            for s in range(3)
+            for q in range(2)
+        )
+        for s, pairs in enumerate(
+            (
+                (mr * fr - mi * fi_, mr * fi_ + mi * fr),
+                (gr * fr + gi * fi_, gi * fr - gr * fi_),
+                (gr * mr + gi * mi, gi * mr - gr * mi),
+            )
+        ):
+            for q in range(2):
+                put(zi, (3 * h + s) * 128, q, pairs[q])
+
+    def back_fine(h):
+        fine(zi, fi, inv_fine, 3 * h * 128, 3 * h * 128 + 384)
+
+    def back_turn(s):
+        his, los = [], []
+        for h in range(2):
+            r0 = (3 * h + s) * 128
+            ir = fi[r0 : r0 + 128, :128]
+            ii = fi[r0 : r0 + 128, 128:]
+            rh, rl = split(ir * tc - ii * ts)
+            ih, il = split(ii * tc + ir * ts)
+            his.append(jnp.concatenate([rh, ih], 0))
+            los.append(jnp.concatenate([rl, il], 0))
+        return jnp.concatenate(his, 1), jnp.concatenate(los, 1)
+
+    def back_coarse(pair, s, z):
+        dh = inv_coarse[:, :256]
+        y = dot(dh, z[0]) + dot(inv_coarse[:, 256:], z[0]) + dot(dh, z[1])
+        for h in range(2):
+            value = y[:, 128 * h : 128 * h + 128] * (1.0 / 16384.0 if s < 2 else 1.0 / 2097152.0)
+            channel = half * 16 + 2 * pair + h
+            if s < 2:
+                own = work[rows(pair, s, h), :]
+                if s == 0:
+                    bias_out[pl.ds(channel, 1), :] = jnp.sum(
+                        own * work[rows(pair, 1, h), :], axis=0, keepdims=True
+                    ) * (1.0 / 128.0)
+                value = value + bias[0, channel] * own
+            work[rows(pair, s, h), :] = value
+
     for s in range(3):
-        x=jnp.concatenate([get(s,0),get(s,1)],1).astype(BF)
-        y=dot(fwd_coarse[...],jnp.concatenate([x,x],0))
-        for h in range(2):
-            yr=y[:128,128*h:128*h+128]; yi=y[128:,128*h:128*h+128]
-            zr=yr*tc+yi*ts; zi=yi*tc-yr*ts
-            r0=(2*s+h)*128
-            for q,z in enumerate((zr,zi)):
-                hi,lo=split(z)
-                zs[r0:r0+128,128*q:128*q+128]=hi
-                zs[r0:r0+128,256+128*q:384+128*q]=lo
-    def fine(w):
-        zh=zs[:,:256]; zl=zs[:,256:]
-        return dot(zh,w[:256])+dot(zh,w[256:])+dot(zl,w[:256])
-    fs[...]=fine(fwd_fine)
+        turn(s, coarse(0, s))
+        spectra(s)
+
+    @pl.loop(0, 7)
+    def _(pair):
+        y0 = coarse(pair + 1, 0)
+        products(0)
+        y1 = coarse(pair + 1, 1)
+        products(1)
+        back_fine(0)
+        turn(0, y0)
+        y2 = coarse(pair + 1, 2)
+        back_fine(1)
+        turn(1, y1)
+        spectra(0)
+        turn(2, y2)
+        z0 = back_turn(0)
+        spectra(1)
+        back_coarse(pair, 0, z0)
+        z1 = back_turn(1)
+        spectra(2)
+        back_coarse(pair, 1, z1)
+        back_coarse(pair, 2, back_turn(2))
+
     for h in range(2):
-        part=lambda s,q: fs[(2*s+h)*128:(2*s+h)*128+128,128*q:128*q+128]
-        mr,mi,gr,gi,fr,fi=part(0,0),part(0,1),part(1,0),part(1,1),part(2,0),part(2,1)
-        prods=((mr*fr-mi*fi,mr*fi+mi*fr),(gr*fr+gi*fi,gi*fr-gr*fi),(gr*mr+gi*mi,gi*mr-gr*mi))
-        for s in range(3):
-            r0=(2*s+h)*128
-            for q in range(2):
-                hi,lo=split(prods[s][q])
-                zs[r0:r0+128,128*q:128*q+128]=hi
-                zs[r0:r0+128,256+128*q:384+128*q]=lo
-    fs[...]=fine(inv_fine)
-    ys=[]
+        products(h)
+        back_fine(h)
     for s in range(3):
-        cols_h=[];cols_l=[]
-        for h in range(2):
-            r0=(2*s+h)*128
-            ir=fs[r0:r0+128,:128]; ii=fs[r0:r0+128,128:]
-            zr=ir*tc-ii*ts; zi=ii*tc+ir*ts
-            rh,rl=split(zr); ih,il=split(zi)
-            cols_h.append(jnp.concatenate([rh,ih],0)); cols_l.append(jnp.concatenate([rl,il],0))
-        zh=jnp.concatenate(cols_h,1); zl=jnp.concatenate(cols_l,1)
-        dh=inv_coarse[:,:256]; dl=inv_coarse[:,256:]
-        ys.append(dot(dh,zh)+dot(dl,zh)+dot(dh,zl))
-    inv_n=1.0/16384.0
-    scale=(inv_n,inv_n,inv_n/128.0)
-    for h in range(2):
-        ch=chunk*16+2*pair+h
-        b=bias[0, ch]
-        m=get(0,h); g=get(1,h)
-        bias_out[pl.ds(ch,1),:]=jnp.sum(m*g,axis=0,keepdims=True)*(1.0/128.0)
-        vals=[ys[s][:,128*h:128*h+128]*scale[s] for s in range(3)]
-        vals[0]=vals[0]+b*m
-        vals[1]=vals[1]+b*g
-        for s in range(3):
-            work[pl.ds(pl.multiple_of(rows(s,h),8),128),:]=vals[s]
+        back_coarse(7, s, back_turn(s))
 
 
 AXES = ("outer", "inner")
@@ -169,7 +221,7 @@
     tabs_in, rest = rest[:6], rest[6:]
     out, bias_out, key, value, query, grad = rest[:6]
     tabs, rest = rest[6:12], rest[12:]
-    filt, packed, recv, back, work, zs, fs, send_in, recv_in, send_out, recv_out, own_out, load = rest
+    filt, packed, recv, back, work, zf, ff, zi, fi, send_in, recv_in, send_out, recv_out, own_out, load = rest
     bias, tabs = tabs[0], tabs[1:]
     me = lax.axis_index("outer") * 16 + lax.axis_index("inner")
     loads = [
@@ -216,10 +268,7 @@
         spread(recv.at[half], work)
 
         with jax.named_scope(f"transforms{half}"):
-
-            @pl.loop(0, 8)
-            def _(pair):
-                transforms(pair, work, bias, bias_out, tabs, zs, fs, half)
+            run_pairs(work, bias, bias_out, tabs, zf, ff, zi, fi, half)
 
         gather(work, back.at[half])
         with jax.named_scope(f"send_out{half}"):
@@ -258,6 +307,8 @@
             pltpu.VMEM((48 * PITCH, 128), F32),
             pltpu.VMEM((768, 512), BF),
             pltpu.VMEM((768, 256), F32),
+            pltpu.VMEM((768, 512), BF),
+            pltpu.VMEM((768, 256), F32),
         ]
         + [pltpu.SemaphoreType.DMA((2,))] * 5
         + [pltpu.SemaphoreType.DMA((11,))],

time: 93.1 us -> 87.6 us (0.941)
  Pallas kernels: 92.3 us -> 86.8 us
    pallas_call x1, Pallas kernels: 88 us -> 82.5 us  [hyena_call(): pl.pallas_call(hyena_kernel, out_shape=(jax.ShapeDtypeStruct((2, DEVICES,...]
where the time goes in v4:
time: 87.6 us; the launch traced here: 87.5 us
  Pallas kernels  86.8 us (99%)
    pallas_call x1, Pallas kernels, hyena_call(): pl.pallas_call(hyena_kernel, out_shape=(jax.ShapeDtypeStruct((2, DEVICES,...  82.5 us
    pallas_call x1, Pallas kernels, finish_call(): pl.pallas_call(finish_kernel, grid=(DEVICES // BLOCK,), out_shape=(rows,...  4.35 us

profile of v4, /device:TPU:1, one launch (start us, length us, event | category | flops | bytes accessed | tf_op | source)
XLA Modules:
  0.0 87.5 jit_solution(13874888355162871796)
XLA Ops:
  0.6 82.5 %hyena.1 = (bf16[2,128,48,128]{3,2,1,0:T(8,128)(2,1)S(1)}, f32[32,128]{1,0:T(8,128)S(1)}, bf16[128,32,128]{2,1,0:T(8,128)(2,1)S(1)}, bf16[128,32,128]{2,1,0:T(8,...) custom-call(bf16[128,32,128]{2,1,0:T(8,128)(2,1)} %bitcast.13, ...), custom_call_target="tpu_custom_call" | custom-call | tf_op jit(solution)/shard_map/hyena/pallas_call | solution.py:291
  83.1 4.3 %finish.1 = (bf16[128,32,128]{2,1,0:T(8,128)(2,1)}, bf16[128,32,128]{2,1,0:T(8,128)(2,1)}, bf16[128,32,128]{2,1,0:T(8,128)(2,1)}, bf16[128,32,128]{2,1,0:T(8,128...) custom-call(bf16[2,128,48,128]{3,2,1,0:T(8,128)(2,1)S(1)} %get-tuple-element.18.back, ...), custom_call_target="tpu_custom_call" | custom-call | tf_op jit(solution)/shard_map/finish/pallas_call | solution.py:349

commit v5 on v4

--- a/solution.py
+++ b/solution.py
@@ -169,6 +169,16 @@
 AXES = ("outer", "inner")
 DEVICES = 128
 BLOCK = 16
+ORDER = (
+    85, 1, 84, 96, 52, 8, 92, 25, 77, 7, 83, 6, 82, 32, 116, 24,
+    76, 97, 53, 2, 86, 3, 87, 33, 117, 9, 93, 39, 114, 5, 81, 15,
+    91, 17, 69, 40, 124, 10, 95, 102, 51, 34, 119, 11, 94, 31, 75, 26,
+    79, 121, 44, 65, 21, 120, 45, 38, 115, 105, 60, 57, 108, 104, 61, 41,
+    125, 14, 90, 30, 74, 35, 118, 99, 54, 56, 109, 4, 80, 27, 78, 64,
+    20, 16, 68, 98, 55, 103, 50, 127, 42, 46, 122, 37, 113, 22, 67, 100,
+    48, 23, 66, 88, 12, 47, 123, 62, 106, 36, 112, 72, 29, 110, 59, 19,
+    71, 89, 13, 43, 126, 111, 58, 28, 73, 70, 18, 107, 63, 101, 49,
+)
 
 
 def partners():
@@ -180,10 +190,9 @@
     zs = [(z + k) % 4 for k in range(4)]
     cores = [(core + k) % 2 for k in range(2)]
     found = []
-    for step in range(1, DEVICES):
-        mixed_step = (step * 47) % DEVICES
-        px, pcore = xs[mixed_step % 4], cores[mixed_step // 4 % 2]
-        py, pz = ys[mixed_step // 8 % 4], zs[mixed_step // 32]
+    for code in ORDER:
+        px, pcore = xs[code // 2 % 4], cores[code % 2]
+        py, pz = ys[code // 8 % 4], zs[code // 32]
         found.append((pz * 2 + py % 2, (py // 2) * 8 + px * 2 + pcore))
     return found
 
@@ -219,19 +228,23 @@
     key_in, value_in, query_in, grad_in, filt_in, *rest,
 ):
     tabs_in, rest = rest[:6], rest[6:]
-    out, bias_out, key, value, query, grad = rest[:6]
-    tabs, rest = rest[6:12], rest[12:]
-    filt, packed, recv, back, work, zf, ff, zi, fi, send_in, recv_in, send_out, recv_out, own_out, load = rest
+    out, bias_out, key, value, query, grad, filt = rest[:7]
+    tabs, rest = rest[7:13], rest[13:]
+    early, packed, recv, back, work, zf, ff, zi, fi, send_in, recv_in, send_out, recv_out, own_out, load = rest
     bias, tabs = tabs[0], tabs[1:]
     me = lax.axis_index("outer") * 16 + lax.axis_index("inner")
+    fields = (
+        (key_in, key), (value_in, value), (grad_in, grad), (query_in, query), (filt_in, filt),
+    )
     loads = [
-        pltpu.make_async_copy(src, dst, load.at[k])
-        for k, (src, dst) in enumerate(
-            (
-                (key_in, key), (value_in, value), (grad_in, grad), (query_in, query), (filt_in, filt),
-                *zip(tabs_in, (bias, *tabs)),
-            )
+        pltpu.make_async_copy(
+            src.at[:, pl.ds(16 * half, 16)], dst.at[:, pl.ds(16 * half, 16)], load.at[5 * half + k]
         )
+        for half in range(2)
+        for k, (src, dst) in enumerate(fields)
+    ] + [
+        pltpu.make_async_copy(src, dst, load.at[10 + k])
+        for k, (src, dst) in enumerate(zip(tabs_in, (bias, *tabs)))
     ]
     for copy in loads:
         copy.start()
@@ -253,34 +266,53 @@
         pl.semaphore_wait(barrier, DEVICES - 1)
     send_all(packed.at[0], recv.at[0], send_in.at[0], recv_in.at[0], me)
     recv[0, me] = packed[0, me]
+    for copy in loads[5:10]:
+        copy.wait()
     with jax.named_scope("gate1"):
         gate(1, key, value, query, grad, filt, packed)
     recv[1, me] = packed[1, me]
     with jax.named_scope("sent_in0"):
         wait_all(packed.at[0], send_in.at[0])
     send_all(packed.at[1], recv.at[1], send_in.at[1], recv_in.at[1], me)
-    for copy in loads[5:]:
+    for copy in loads[10:]:
         copy.wait()
-    own_back = []
     for half in range(2):
         with jax.named_scope(f"wait_in{half}"):
             wait_all(recv.at[half], recv_in.at[half])
         spread(recv.at[half], work)
-
         with jax.named_scope(f"transforms{half}"):
             run_pairs(work, bias, bias_out, tabs, zf, ff, zi, fi, half)
-
         gather(work, back.at[half])
         with jax.named_scope(f"send_out{half}"):
-            send_all(back.at[half], out.at[half], send_out.at[half], recv_out.at[half], me)
-        own_back.append(pltpu.make_async_copy(back.at[half, me], out.at[half, me], own_out.at[half]))
-        own_back[half].start()
+            home = early if half == 0 else out
+            send_all(back.at[half], home, send_out.at[half], recv_out.at[half], me)
+    own = pltpu.make_async_copy(back.at[1, me], out.at[me], own_out)
+    own.start()
+    early[me] = back[0, me]
+    with jax.named_scope("wait_out0"):
+        wait_all(early, recv_out.at[0])
+    with jax.named_scope("finish0"):
+        settle(early, key, value, query, grad, filt)
     wait_all(packed.at[1], send_in.at[1])
     for half in range(2):
-        own_back[half].wait()
         wait_all(back.at[half], send_out.at[half])
-        with jax.named_scope(f"wait_out{half}"):
-            wait_all(out.at[half], recv_out.at[half])
+    own.wait()
+    with jax.named_scope("wait_out1"):
+        wait_all(out, recv_out.at[1])
+
+
+def settle(early, key, value, query, grad, filt):
+    @pl.loop(0, DEVICES // 8)
+    def _(group):
+        at = pl.ds(pl.multiple_of(group * 8, 8), 8)
+        rows = (at, slice(0, 16))
+        convolved = early[at, :16].astype(F32)
+        mixed_grad = early[at, 16:32].astype(F32)
+        query[rows] = (query[rows].astype(F32) * convolved).astype(BF)
+        grad[rows] = (grad[rows].astype(F32) * convolved).astype(BF)
+        value[rows] = (value[rows].astype(F32) * mixed_grad).astype(BF)
+        key[rows] = (key[rows].astype(F32) * mixed_grad).astype(BF)
+        filt[rows] = early[at, 32:].astype(F32)
 
 
 def hyena_call(bias, key, value, query, grad, filt):
@@ -291,16 +323,17 @@
     return pl.pallas_call(
         hyena_kernel,
         out_shape=(
-            jax.ShapeDtypeStruct((2, DEVICES, 48, 128), BF),
+            jax.ShapeDtypeStruct((DEVICES, 48, 128), BF),
             jax.ShapeDtypeStruct((32, 128), F32),
             rows, rows, rows, rows,
+            jax.ShapeDtypeStruct((DEVICES, 32, 128), F32),
         ),
         in_specs=[hbm] * 11,
-        out_specs=(hbm,) + (vmem,) * 5,
+        out_specs=(hbm,) + (vmem,) * 6,
         scratch_shapes=[pltpu.SMEM((1, 32), F32)]
         + [pltpu.VMEM(t.shape, t.dtype) for t in consts]
         + [
-            pltpu.VMEM((DEVICES, 32, 128), F32),
+            pltpu.VMEM((DEVICES, 48, 128), BF),
             pltpu.VMEM((2, DEVICES, 48, 128), BF),
             pltpu.VMEM((2, DEVICES, 48, 128), BF),
             pltpu.VMEM((2, DEVICES, 48, 128), BF),
@@ -310,10 +343,11 @@
             pltpu.VMEM((768, 512), BF),
             pltpu.VMEM((768, 256), F32),
         ]
-        + [pltpu.SemaphoreType.DMA((2,))] * 5
-        + [pltpu.SemaphoreType.DMA((11,))],
+        + [pltpu.SemaphoreType.DMA((2,))] * 4
+        + [pltpu.SemaphoreType.DMA]
+        + [pltpu.SemaphoreType.DMA((16,))],
         compiler_params=pltpu.CompilerParams(
-            collective_id=0, has_side_effects=True, vmem_limit_bytes=40 * 2**20
+            collective_id=0, has_side_effects=True, vmem_limit_bytes=36 * 2**20
         ),
         name="hyena",
     )(
@@ -324,34 +358,42 @@
     )
 
 
-def finish_kernel(back, bias_rows, key, value, query, grad, output, query_grad, key_grad, value_grad, filter_grad, bias_grad):
-    step = pl.program_id(0)
-    at = pl.ds(pl.multiple_of(step * BLOCK, BLOCK), BLOCK)
-    for half in range(2):
-        rows = slice(16 * half, 16 * half + 16)
-        convolved = back[half, at, :16].astype(F32)
-        mixed_grad = back[half, at, 16:32].astype(F32)
-        output[:, rows] = (query[at, rows].astype(F32) * convolved).astype(BF)
-        query_grad[:, rows] = (grad[at, rows].astype(F32) * convolved).astype(BF)
-        key_grad[:, rows] = (value[at, rows].astype(F32) * mixed_grad).astype(BF)
-        value_grad[:, rows] = (key[at, rows].astype(F32) * mixed_grad).astype(BF)
-        filter_grad[:, rows] = back[half, at, 32:].astype(F32)
-
-    @pl.when(step == 0)
-    def _():
-        bias_grad[...] = jnp.sum(bias_rows[...].T, axis=0, keepdims=True)
+def finish_kernel(late, bias_rows, key, value, query, grad, filt, *rest):
+    outs, bias_grad, bufs, sems = rest[:5], rest[5], rest[6:11], rest[11]
+    first, second = pl.ds(0, 16), pl.ds(16, 16)
+    for k, done in enumerate((query, grad, value, key, filt)):
+        pltpu.make_async_copy(done.at[:, first], outs[k].at[:, first], sems.at[k]).start()
+
+    @pl.loop(0, DEVICES // BLOCK)
+    def _(group):
+        at = pl.ds(pl.multiple_of(group * BLOCK, BLOCK), BLOCK)
+        convolved = late[at, :16].astype(F32)
+        mixed_grad = late[at, 16:32].astype(F32)
+        bufs[0][at] = (query[at, second].astype(F32) * convolved).astype(BF)
+        bufs[1][at] = (grad[at, second].astype(F32) * convolved).astype(BF)
+        bufs[2][at] = (value[at, second].astype(F32) * mixed_grad).astype(BF)
+        bufs[3][at] = (key[at, second].astype(F32) * mixed_grad).astype(BF)
+        bufs[4][at] = late[at, 32:].astype(F32)
+        for k in range(5):
+            pltpu.make_async_copy(bufs[k].at[at], outs[k].at[at, second], sems.at[k]).start()
+
+    bias_grad[...] = jnp.sum(bias_rows[...].T, axis=0, keepdims=True)
+    for k in range(5):
+        pltpu.make_async_copy(outs[k], outs[k], sems.at[k]).wait()
 
 
 def finish_call(*args):
     vmem = pl.BlockSpec(memory_space=pltpu.VMEM)
-    block = pl.BlockSpec((BLOCK, 32, 128), lambda i: (i, 0, 0))
-    rows = jax.ShapeDtypeStruct((DEVICES, 32, 128), BF)
+    hbm = pl.BlockSpec(memory_space=pltpu.HBM)
+    types = (BF, BF, BF, BF, F32)
     return pl.pallas_call(
         finish_kernel,
-        grid=(DEVICES // BLOCK,),
-        out_shape=(rows, rows, rows, rows, jax.ShapeDtypeStruct((DEVICES, 32, 128), F32), jax.ShapeDtypeStruct((1, 32), F32)),
-        in_specs=[vmem] * 6,
-        out_specs=(block,) * 5 + (pl.BlockSpec((1, 32), lambda i: (0, 0)),),
+        out_shape=tuple(jax.ShapeDtypeStruct((DEVICES, 32, 128), t) for t in types)
+        + (jax.ShapeDtypeStruct((1, 32), F32),),
+        in_specs=[vmem] * 7,
+        out_specs=(hbm,) * 5 + (vmem,),
+        scratch_shapes=[pltpu.VMEM((DEVICES, 16, 128), t) for t in types]
+        + [pltpu.SemaphoreType.DMA((5,))],
         compiler_params=pltpu.CompilerParams(vmem_limit_bytes=16 * 2**20),
         name="finish",
     )(*args)
@@ -361,10 +403,10 @@
     def rows(array):
         return array.reshape(DEVICES, 32, 128)
 
-    back, bias_rows, key, value, query, grad = hyena_call(
+    kept = hyena_call(
         skip_bias, rows(key_proj), rows(value_proj), rows(query_gate), rows(out_grad), rows(filters)
     )
-    *grads, bias_grad = finish_call(back, bias_rows, key, value, query, grad)
+    *grads, bias_grad = finish_call(*kept)
     return (*[array.reshape(-1, 128) for array in grads], bias_grad.reshape(-1))
 
 

time: 87.6 us -> 86.1 us (0.983)
  Pallas kernels: 86.8 us -> 85.4 us
    pallas_call x2, Pallas kernels: 86.8 us -> 85.4 us  [the longest x1 82.2 us: hyena_call(): pl.pallas_call(hyena_kernel, out_shape=(jax.ShapeDtypeStruct((DEVICES, 48...]
where the time goes in v5:
time: 86.1 us; the launch traced here: 86 us
  Pallas kernels  85.4 us (99%)
    pallas_call x1, Pallas kernels, hyena_call(): pl.pallas_call(hyena_kernel, out_shape=(jax.ShapeDtypeStruct((DEVICES, 48...  82.2 us
    pallas_call x1, Pallas kernels, finish_call(): pl.pallas_call(finish_kernel, out_shape=tuple((jax.ShapeDtypeStruct((DEVI...  3.17 us

profile of v5, /device:TPU:1, one launch (start us, length us, event | category | flops | bytes accessed | tf_op | source)
XLA Modules:
  0.0 86.0 jit_solution(13734664308135959836)
XLA Ops:
  0.6 82.2 %hyena.1 = (bf16[128,48,128]{2,1,0:T(8,128)(2,1)S(1)}, f32[32,128]{1,0:T(8,128)S(1)}, bf16[128,32,128]{2,1,0:T(8,128)(2,1)S(1)}, bf16[128,32,128]{2,1,0:T(8,128)...) custom-call(bf16[128,32,128]{2,1,0:T(8,128)(2,1)} %bitcast.13, ...), custom_call_target="tpu_custom_call" | custom-call | tf_op jit(solution)/shard_map/hyena/pallas_call | solution.py:323
  82.8 3.2 %finish.1 = (bf16[128,32,128]{2,1,0:T(8,128)(2,1)}, bf16[128,32,128]{2,1,0:T(8,128)(2,1)}, bf16[128,32,128]{2,1,0:T(8,128)(2,1)}, bf16[128,32,128]{2,1,0:T(8,128...) custom-call(bf16[128,48,128]{2,1,0:T(8,128)(2,1)S(1)} %get-tuple-element.19.late, ...), custom_call_target="tpu_custom_call" | custom-call | tf_op jit(solution)/shard_map/finish/pallas_call | solution.py:389

commit v6 on v5

--- a/solution.py
+++ b/solution.py
@@ -337,7 +337,7 @@
             pltpu.VMEM((2, DEVICES, 48, 128), BF),
             pltpu.VMEM((2, DEVICES, 48, 128), BF),
             pltpu.VMEM((2, DEVICES, 48, 128), BF),
-            pltpu.VMEM((48 * PITCH, 128), F32),
+            pltpu.VMEM((49 * PITCH, 128), F32),
             pltpu.VMEM((768, 512), BF),
             pltpu.VMEM((768, 256), F32),
             pltpu.VMEM((768, 512), BF),

time: 86.1 us -> 86.1 us (level)
  no operation moved by 1% of the time
where the time goes in v6:
time: 86.1 us; the launch traced here: 86 us
  Pallas kernels  85.4 us (99%)
    pallas_call x1, Pallas kernels, hyena_call(): pl.pallas_call(hyena_kernel, out_shape=(jax.ShapeDtypeStruct((DEVICES, 48...  82.2 us
    pallas_call x1, Pallas kernels, finish_call(): pl.pallas_call(finish_kernel, out_shape=tuple((jax.ShapeDtypeStruct((DEVI...  3.17 us

profile of v6, /device:TPU:1, one launch (start us, length us, event | category | flops | bytes accessed | tf_op | source)
XLA Modules:
  0.0 86.0 jit_solution(4709256605273162115)
XLA Ops:
  0.6 82.2 %hyena.1 = (bf16[128,48,128]{2,1,0:T(8,128)(2,1)S(1)}, f32[32,128]{1,0:T(8,128)S(1)}, bf16[128,32,128]{2,1,0:T(8,128)(2,1)S(1)}, bf16[128,32,128]{2,1,0:T(8,128)...) custom-call(bf16[128,32,128]{2,1,0:T(8,128)(2,1)} %bitcast.13, ...), custom_call_target="tpu_custom_call" | custom-call | tf_op jit(solution)/shard_map/hyena/pallas_call | solution.py:323
  82.9 3.2 %finish.1 = (bf16[128,32,128]{2,1,0:T(8,128)(2,1)}, bf16[128,32,128]{2,1,0:T(8,128)(2,1)}, bf16[128,32,128]{2,1,0:T(8,128)(2,1)}, bf16[128,32,128]{2,1,0:T(8,128...) custom-call(bf16[128,48,128]{2,1,0:T(8,128)(2,1)S(1)} %get-tuple-element.19.late, ...), custom_call_target="tpu_custom_call" | custom-call | tf_op jit(solution)/shard_map/finish/pallas_call | solution.py:389

commit v7 on v6

--- a/solution.py
+++ b/solution.py
@@ -169,6 +169,7 @@
 AXES = ("outer", "inner")
 DEVICES = 128
 BLOCK = 16
+HEAD = 112
 ORDER = (
     85, 1, 84, 96, 52, 8, 92, 25, 77, 7, 83, 6, 82, 32, 116, 24,
     76, 97, 53, 2, 86, 3, 87, 33, 117, 9, 93, 39, 114, 5, 81, 15,
@@ -197,20 +198,20 @@
     return found
 
 
-def send_all(src, dst, send_sem, recv_sem, me):
-    for outer, inner in partners():
+def send_all(src, dst, send_sem, recv_sem, me, tail_sem=None):
+    for k, (outer, inner) in enumerate(partners()):
         pltpu.make_async_remote_copy(
             src_ref=src.at[outer * 16 + inner],
             dst_ref=dst.at[me],
-            send_sem=send_sem,
+            send_sem=send_sem if tail_sem is None or k < HEAD else tail_sem,
             recv_sem=recv_sem,
             device_id={"outer": outer, "inner": inner},
             device_id_type=pl.DeviceIdType.MESH,
         ).start()
 
 
-def wait_all(buf, sem):
-    rest = buf.at[pl.ds(0, DEVICES - 1)]
+def wait_all(buf, sem, count=DEVICES - 1):
+    rest = buf.at[pl.ds(0, count)]
     pltpu.make_async_copy(rest, rest, sem).wait()
 
 
@@ -264,7 +265,7 @@
         gate(0, key, value, query, grad, filt, packed)
     with jax.named_scope("bar_wait"):
         pl.semaphore_wait(barrier, DEVICES - 1)
-    send_all(packed.at[0], recv.at[0], send_in.at[0], recv_in.at[0], me)
+    send_all(packed.at[0], recv.at[0], send_in.at[0], recv_in.at[0], me, send_in.at[2])
     recv[0, me] = packed[0, me]
     for copy in loads[5:10]:
         copy.wait()
@@ -272,7 +273,7 @@
         gate(1, key, value, query, grad, filt, packed)
     recv[1, me] = packed[1, me]
     with jax.named_scope("sent_in0"):
-        wait_all(packed.at[0], send_in.at[0])
+        wait_all(packed.at[0], send_in.at[0], HEAD)
     send_all(packed.at[1], recv.at[1], send_in.at[1], recv_in.at[1], me)
     for copy in loads[10:]:
         copy.wait()
@@ -293,6 +294,7 @@
         wait_all(early, recv_out.at[0])
     with jax.named_scope("finish0"):
         settle(early, key, value, query, grad, filt)
+    wait_all(packed.at[0], send_in.at[2], DEVICES - 1 - HEAD)
     wait_all(packed.at[1], send_in.at[1])
     for half in range(2):
         wait_all(back.at[half], send_out.at[half])
@@ -343,7 +345,7 @@
             pltpu.VMEM((768, 512), BF),
             pltpu.VMEM((768, 256), F32),
         ]
-        + [pltpu.SemaphoreType.DMA((2,))] * 4
+        + [pltpu.SemaphoreType.DMA((3,))] * 4
         + [pltpu.SemaphoreType.DMA]
         + [pltpu.SemaphoreType.DMA((16,))],
         compiler_params=pltpu.CompilerParams(

time: 86.1 us -> 85.8 us (level)
  no operation moved by 1% of the time
where the time goes in v7:
time: 85.8 us; the launch traced here: 85.7 us
  Pallas kernels  85.1 us (99%)
    pallas_call x1, Pallas kernels, hyena_call(): pl.pallas_call(hyena_kernel, out_shape=(jax.ShapeDtypeStruct((DEVICES, 48...  81.9 us
    pallas_call x1, Pallas kernels, finish_call(): pl.pallas_call(finish_kernel, out_shape=tuple((jax.ShapeDtypeStruct((DEVI...  3.17 us

profile of v7, /device:TPU:1, one launch (start us, length us, event | category | flops | bytes accessed | tf_op | source)
XLA Modules:
  0.0 85.7 jit_solution(9848386489628901966)
XLA Ops:
  0.6 81.9 %hyena.1 = (bf16[128,48,128]{2,1,0:T(8,128)(2,1)S(1)}, f32[32,128]{1,0:T(8,128)S(1)}, bf16[128,32,128]{2,1,0:T(8,128)(2,1)S(1)}, bf16[128,32,128]{2,1,0:T(8,128)...) custom-call(bf16[128,32,128]{2,1,0:T(8,128)(2,1)} %bitcast.13, ...), custom_call_target="tpu_custom_call" | custom-call | tf_op jit(solution)/shard_map/hyena/pallas_call | solution.py:325
  82.5 3.2 %finish.1 = (bf16[128,32,128]{2,1,0:T(8,128)(2,1)}, bf16[128,32,128]{2,1,0:T(8,128)(2,1)}, bf16[128,32,128]{2,1,0:T(8,128)(2,1)}, bf16[128,32,128]{2,1,0:T(8,128...) custom-call(bf16[128,48,128]{2,1,0:T(8,128)(2,1)S(1)} %get-tuple-element.19.late, ...), custom_call_target="tpu_custom_call" | custom-call | tf_op jit(solution)/shard_map/finish/pallas_call | solution.py:391
